TPU v7x, 256 devices: a whole 4x4x8 slice. The times are simulated.
256 devices in a mesh: ep: 64 (over x, z, core), tp: 4 (over y).
Axes of the slice: x: 4, y: 4, z: 8, core: 2. Of those that a mesh axis runs over, the one named last changes fastest.
Arguments:
- tokens: bfloat16 [2048, 7168], P('ep', 'tp'), may hold values from -6 to 6
- routes: int32 [2048, 8], P('ep'), may hold values from 0 to 63, all different within a row; in each aligned block of 32 rows (0 to 31, 32 to 63, ...) at most 8 rows name the same one
- route_weights: float32 [2048, 8], P('ep'), may hold values from 0.05 to 1
- gate_proj: bfloat16 [64, 7168, 1024], P('ep', None, 'tp'), may hold values from -0.0625 to 0.0625
- up_proj: bfloat16 [64, 7168, 1024], P('ep', None, 'tp'), may hold values from -0.0625 to 0.0625
- down_proj: bfloat16 [64, 1024, 7168], P('ep', 'tp'), may hold values from -0.1875 to 0.1875
Outputs:
- mixed: bfloat16 [2048, 7168], P('ep', 'tp')
Inputs may be any that keep to these rules, and one draw needn't show every extreme that they name: `routes`: each token names 8 different experts; among the 32 tokens of one index of ep no expert is named more than 8 times.
All inputs are finite; a program needn't handle non-finite values.
Results may differ from a plain program's by a relative error of at most 0.012.
Values may be sent and summed in bfloat16 or wider, within the bound.
No kernel may reach another device: no remote copies, remote signals or barrier semaphores. Data moves between devices by JAX's collectives and lax.ppermute only.
A program may use at most 64 MiB of HBM per device.

v0:
```python
import jax
import jax.numpy as jnp
from jax import lax
from jax.sharding import PartitionSpec as P


def per_device(tokens, routes, route_weights, gate_proj, up_proj, down_proj):
    w_gate = gate_proj[0]
    w_up = up_proj[0]
    w_down = down_proj[0]
    tok_count = tokens.shape[0]
    fanout = routes.shape[1]
    experts = lax.axis_size("ep")
    capacity = min(tok_count, max(2, 2 * tok_count * fanout // experts))
    slot_count = experts * capacity
    flat_ids = routes.reshape(-1)
    onehot = (flat_ids[:, None] == jnp.arange(experts, dtype=jnp.int32)[None, :]).astype(jnp.int32)
    before = jnp.cumsum(onehot, axis=0) - onehot
    position = jnp.sum(before * onehot, axis=1)
    target = flat_ids * capacity + position
    select = jnp.any(
        target.reshape(tok_count, fanout)[None, :, :]
        == jnp.arange(slot_count, dtype=jnp.int32)[:, None, None],
        axis=2,
    ).astype(jnp.bfloat16)
    sending = jnp.dot(select, tokens, preferred_element_type=jnp.float32).astype(jnp.bfloat16)
    arrived = lax.all_to_all(sending, "ep", split_axis=0, concat_axis=0, tiled=True)
    block_in = lax.all_gather(arrived, "tp", axis=1, tiled=True)
    gate_act = jnp.dot(block_in, w_gate, preferred_element_type=jnp.float32)
    up_act = jnp.dot(block_in, w_up, preferred_element_type=jnp.float32)
    hidden = (jax.nn.silu(gate_act) * up_act).astype(jnp.bfloat16)
    partial_value = jnp.dot(hidden, w_down, preferred_element_type=jnp.float32)
    summed = lax.psum_scatter(
        partial_value.astype(jnp.bfloat16), "tp", scatter_dimension=1, tiled=True
    )
    back_rows = lax.all_to_all(summed, "ep", split_axis=0, concat_axis=0, tiled=True)
    picked = jnp.take(back_rows, target, axis=0).astype(jnp.float32)
    weighted = picked * route_weights.reshape(-1)[:, None]
    mixed = jnp.sum(weighted.reshape(tok_count, fanout, -1), axis=1)
    return mixed.astype(jnp.bfloat16)


def solution(mesh):
    in_specs = (
        P("ep", "tp"),
        P("ep", None),
        P("ep", None),
        P("ep", None, "tp"),
        P("ep", None, "tp"),
        P("ep", "tp", None),
    )
    out_specs = P("ep", "tp")
    return jax.shard_map(
        per_device, mesh=mesh, in_specs=in_specs, out_specs=out_specs, check_vma=False
    )
```

profile of v0, /device:TPU:1, one launch (start us, length us, event | category | flops | bytes accessed | tf_op | source)
XLA Modules:
  0.0 306.0 jit_solution(914386068358793385)
XLA Ops:
  6.5 0.0 copy-start
  6.5 0.0 all-gather.2.cloned.1.call-start
  6.5 0.8 copy.15
  7.3 0.1 eq.39
  7.4 0.1 reshape.78
  7.5 0.6 reduce-window.6
  8.1 0.2 slice_reduce_fusion
  8.4 0.1 fusion.18
  8.5 0.1 reduce_sum.23
  8.6 0.2 fusion.12
  8.8 0.0 copy-done
  8.8 0.7 fusion.5
  9.5 58.3 %all_to_all.24 = bf16[64,8,1792]{2,1,0:T(8,128)(2,1)} all-to-all(bf16[64,8,1792]{2,1,0:T(8,128)(2,1)S(1)} %fusion.5), channel_id=1, replica_groups=mesh['ep'=64,'tp'=4] {'ep'}, dimensions={0} | all-to-all | bytes 3670016 | tf_op jit(solution)/shard_map/all_to_all | solution.py:27
  67.8 0.0 all-gather.2.cloned.1.call-update
  67.8 0.0 reduce-scatter.2.cloned.1.call-start
  67.9 73.7 %all-gather.2.cloned.1.call-done = bf16[512,7168]{1,0:T(8,128)(2,1)} async-done(((bf16[512,1792]{1,0:T(8,128)(2,1)}), bf16[512,7168]{1,0:T(8,128)(2,1)}) %all-gather.2.cloned.1.call-update) | async-done | bytes 7340048 | tf_op jit(solution)/shard_map/all_gather | solution.py:28
  141.6 6.2 %fusion.3 = f32[512,256]{1,0:T(8,128)S(1)} fusion(bf16[512,7168]{1,0:T(8,128)(2,1)} %all-gather.2.cloned.1.call-done, bf16[1,7168,256]{2,1,0:T(8,128)(2,1)} %param.9), kind=kOutput, calls=%fused_computation.5 | convolution fusion | flops 1879048192 | bytes 11534336 | tf_op jit(solution)/shard_map/dot_general | solution.py:29
  147.7 16.0 %convolution_convert_fusion = bf16[512,7168]{1,0:T(8,128)(2,1)} fusion(bf16[1,256,7168]{2,1,0:T(8,128)(2,1)} %param.11, bf16[512,7168]{1,0:T(8,128)(2,1)} %all-gather.2.cloned.1.call-done, bf16[1,7168,256]{2,1,0:T(8,128)(2,1)} %param.10, f32[512,256]{1,0:T(8,128)S(1)} %fusion.3), kind=kOutput, calls=%fused_computation.1 | convolution fusion | flops 3762552832 | bytes 22544384 | tf_op jit(solution)/shard_map/dot_general | solution.py:32
  163.8 0.0 reduce-scatter.2.cloned.1.call-update
  163.8 0.0 copy-start.1
  163.8 76.2 %reduce-scatter.2.cloned.1.call-done = bf16[512,1792]{1,0:T(8,128)(2,1)} async-done(((bf16[512,7168]{1,0:T(8,128)(2,1)}), bf16[512,1792]{1,0:T(8,128)(2,1)}) %reduce-scatter.2.cloned.1.call-update) | async-done | bytes 1835024 | tf_op jit(solution)/shard_map/reduce_scatter | solution.py:33
  240.0 10.7 %all-to-all-start.1 = ((bf16[64,8,1792]{2,1,0:T(8,128)(2,1)}), bf16[64,8,1792]{2,1,0:T(8,128)(2,1)S(1)}, u32[]{:S(2)}, u32[]{:S(2)}) async-start(bf16[64,8,1792]{2,1,0:T(8,128)(2,1)} %bitcast.51), calls=%async_computation.2 | async-start | bytes 3670016 | tf_op jit(solution)/shard_map/all_to_all | solution.py:36
  250.7 0.1 mul.45
  250.8 0.0 copy-done.1
  250.8 0.1 copy.19
  250.9 45.2 %all-to-all-done.1 = bf16[64,8,1792]{2,1,0:T(8,128)(2,1)S(1)} async-done(((bf16[64,8,1792]{2,1,0:T(8,128)(2,1)}), bf16[64,8,1792]{2,1,0:T(8,128)(2,1)S(1)}, u32[]{:S(2)}, u32[]{:S(2)}) %all-to-all-start.1) | async-done | bytes 1835040 | tf_op jit(solution)/shard_map/all_to_all | solution.py:36
  296.1 1.3 gather_fusion
  297.4 1.7 multiply_reduce_fusion
  (7 shorter events, 0.1 us)
Async XLA Ops:
  6.5 2.3 copy-start
  6.5 135.0 %all-gather.2.cloned.1.call-start = ((), (), s32[]{:S(2)}) async-start(), calls=%async_computation.3 | async-start | bytes 9175040 | tf_op jit(solution)/shard_map/all_gather | solution.py:28
  67.8 172.1 %reduce-scatter.2.cloned.1.call-start = ((), (), s32[]{:S(2)}) async-start(), calls=%async_computation.4 | async-start | bytes 9175040 | tf_op jit(solution)/shard_map/reduce_scatter | solution.py:33
  163.8 87.0 %copy-start.1 = (f32[32,8]{0,1:T(8,128)S(1)}, f32[32,8]{0,1:T(8,128)}, u32[]{:S(2)}) copy-start(f32[32,8]{0,1:T(8,128)} %param.8) | copy-start | bytes 3076
  240.0 56.1 %all-to-all-start.1 = ((bf16[64,8,1792]{2,1,0:T(8,128)(2,1)}), bf16[64,8,1792]{2,1,0:T(8,128)(2,1)S(1)}, u32[]{:S(2)}, u32[]{:S(2)}) async-start(bf16[64,8,1792]{2,1,0:T(8,128)(2,1)} %bitcast.51), calls=%async_computation.2 | async-start | bytes 3670016 | tf_op jit(solution)/shard_map/all_to_all | solution.py:36
Sparse Core Ops, SparseCore 0:
  67.9 73.5 all-gather.1
  163.9 76.0 reduce-scatter.1
where the time goes:
time: 306 us
  waiting for transfers between devices  195 us (64%)
  blocking collectives  58.3 us (19%)
  matrix products  22.9 us (7%)
  between operations  13.5 us (4%)
  starting transfers between devices  10.8 us (4%)
    reduce_scatter x1, waiting for transfers between devices, per_device(): lax.psum_scatter(partial_value.astype(jnp.bfloat16), 'tp', scatter_dimens...  76.2 us
    all_gather x1, waiting for transfers between devices, per_device(): block_in = lax.all_gather(arrived, 'tp', axis=1, tiled=True)  73.7 us
    all_to_all x1, blocking collectives, per_device(): lax.all_to_all(sending, 'ep', split_axis=0, concat_axis=0, tiled=True)  58.3 us
    all_to_all x1, waiting for transfers between devices, per_device(): lax.all_to_all(summed, 'ep', split_axis=0, concat_axis=0, tiled=True)  45.2 us
    dot_general x1, matrix products, per_device(): partial_value = jnp.dot(hidden, w_down, preferred_element_type=jnp.float32)  16 us
    all_to_all x1, starting transfers between devices, per_device(): lax.all_to_all(summed, 'ep', split_axis=0, concat_axis=0, tiled=True)  10.7 us
    dot_general x1, matrix products, per_device(): gate_act = jnp.dot(block_in, w_gate, preferred_element_type=jnp.float32)  6.18 us
  transfers between devices with their start and end apart: 3, of which 3 were waited for; matrix products, arithmetic and copies ran while one was open for 0% of the time, Pallas kernels for 0%

commit v1 on v0

v1 whole, which is shorter than its diff:
```python
import jax
import jax.numpy as jnp
from jax import lax
from jax.experimental import pallas as pl
from jax.experimental.pallas import tpu as pltpu
from jax.sharding import PartitionSpec as P

CHUNKS = 2


def hidden_kernel(x_ref, gate_ref, up_ref, out_ref, gate_acc, up_acc):
    step = pl.program_id(0)

    @pl.when(step == 0)
    def _():
        gate_acc[...] = jnp.zeros_like(gate_acc)
        up_acc[...] = jnp.zeros_like(up_acc)

    gate_acc[...] += jnp.dot(x_ref[...], gate_ref[...], preferred_element_type=jnp.float32)
    up_acc[...] += jnp.dot(x_ref[...], up_ref[...], preferred_element_type=jnp.float32)

    @pl.when(step == pl.num_programs(0) - 1)
    def _():
        gate = gate_acc[...]
        out_ref[...] = (gate / (1.0 + jnp.exp(-gate)) * up_acc[...]).astype(out_ref.dtype)


def hidden_of(block_in, gate_proj, up_proj):
    rows, width = block_in.shape
    cols = gate_proj.shape[2]
    steps = 4
    depth = width // steps
    weight = pl.BlockSpec((None, depth, cols), lambda k: (0, k, 0))
    return pl.pallas_call(
        hidden_kernel,
        grid=(steps,),
        in_specs=[pl.BlockSpec((rows, depth), lambda k: (0, k)), weight, weight],
        out_specs=pl.BlockSpec((rows, cols), lambda k: (0, 0)),
        out_shape=jax.ShapeDtypeStruct((rows, cols), jnp.bfloat16),
        scratch_shapes=[pltpu.VMEM((rows, cols), jnp.float32)] * 2,
        cost_estimate=pl.CostEstimate(
            flops=4 * rows * width * cols,
            bytes_accessed=2 * rows * width + 4 * width * cols,
            transcendentals=rows * cols,
        ),
        name="hidden",
    )(block_in, gate_proj, up_proj)


def down_kernel(*refs):
    out_ref = refs[-1]
    pairs = (len(refs) - 1) // 2
    total = jnp.dot(refs[0][...], refs[pairs][...], preferred_element_type=jnp.float32)
    for i in range(1, pairs):
        total += jnp.dot(refs[i][...], refs[pairs + i][...], preferred_element_type=jnp.float32)
    out_ref[...] = total.astype(out_ref.dtype)


def down_of(hiddens, downs):
    rows, inner = hiddens[0].shape
    width = downs[0].shape[1]
    steps = 7
    cols = width // steps
    n = len(hiddens)
    return pl.pallas_call(
        down_kernel,
        grid=(steps,),
        in_specs=[pl.BlockSpec((rows, inner), lambda k: (0, 0))] * n
        + [pl.BlockSpec((inner, cols), lambda k: (0, k))] * n,
        out_specs=pl.BlockSpec((rows, cols), lambda k: (0, k)),
        out_shape=jax.ShapeDtypeStruct((rows, width), jnp.bfloat16),
        cost_estimate=pl.CostEstimate(
            flops=2 * n * rows * inner * width,
            bytes_accessed=2 * n * inner * (rows + width) + 2 * rows * width,
            transcendentals=0,
        ),
        name="down",
    )(*hiddens, *downs)


def layer(tokens, routes, route_weights, gate_proj, up_proj, down_proj):
    w_down = down_proj[0]
    tok_count, width = tokens.shape
    fanout = routes.shape[1]
    experts = lax.axis_size("ep")
    parts = lax.axis_size("tp")
    me = lax.axis_index("tp")
    capacity = min(tok_count, max(2, 2 * tok_count * fanout // experts))
    share = capacity // CHUNKS

    def shift(value, by):
        return lax.ppermute(value, "tp", [(i, (i + by) % parts) for i in range(parts)])

    downs = []
    for by in range(parts):
        start = lax.rem(me + by, parts) * width
        piece = lax.dynamic_slice_in_dim(w_down, start, width, axis=1)
        downs.append(piece if by == 0 else shift(piece, by))

    flat_ids = routes.reshape(-1)
    onehot = (flat_ids[:, None] == jnp.arange(experts, dtype=jnp.int32)[None, :]).astype(jnp.int32)
    before = jnp.cumsum(onehot, axis=0) - onehot
    position = jnp.sum(before * onehot, axis=1)
    target = (flat_ids * capacity + position).reshape(tok_count, fanout)

    mixed = jnp.zeros((tok_count, width), jnp.float32)
    for chunk in range(CHUNKS):
        rows = experts * share
        row = jnp.arange(rows, dtype=jnp.int32)
        slot = row // share * capacity + chunk * share + row % share
        select = jnp.any(target[None, :, :] == slot[:, None, None], axis=2).astype(jnp.bfloat16)
        sending = jnp.dot(select, tokens, preferred_element_type=jnp.float32).astype(jnp.bfloat16)
        arrived = lax.all_to_all(
            sending.reshape(experts, share, width), "ep", split_axis=0, concat_axis=0, tiled=True
        )
        arrived = arrived.reshape(rows, width)
        block_in = lax.all_gather(arrived, "tp", axis=1, tiled=True)
        hidden = hidden_of(block_in, gate_proj, up_proj)
        hiddens = [hidden] + [shift(hidden, by) for by in range(1, parts)]
        out = down_of(hiddens, downs)
        back = lax.all_to_all(
            out.reshape(experts, share, width), "ep", split_axis=0, concat_axis=0, tiled=True
        ).reshape(rows, width)
        weight = jnp.sum(
            jnp.where(target[:, :, None] == slot[None, None, :], route_weights[:, :, None], 0.0), axis=1
        )
        high = weight.astype(jnp.bfloat16)
        low = (weight - high.astype(jnp.float32)).astype(jnp.bfloat16)
        both = jnp.dot(jnp.concatenate([high, low]), back, preferred_element_type=jnp.float32)
        mixed = mixed + (both[:tok_count] + both[tok_count:])
    return mixed.astype(jnp.bfloat16)


def solution(mesh):
    in_specs = (
        P("ep", "tp"),
        P("ep", None),
        P("ep", None),
        P("ep", None, "tp"),
        P("ep", None, "tp"),
        P("ep", "tp", None),
    )
    out_specs = P("ep", "tp")
    return jax.shard_map(layer, mesh=mesh, in_specs=in_specs, out_specs=out_specs, check_vma=False)
```

time: 306 us -> 251 us (0.82)
  waiting for transfers between devices: 195 us -> 85.4 us
  Pallas kernels: 0 us -> 26.5 us
  starting transfers between devices: 10.8 us -> 36.2 us
  matrix products: 22.9 us -> 1.46 us
  local copies, waits for them, and re-layouts: 2.76 us -> 14.8 us
  blocking collectives: 58.3 us -> 70.2 us
    reduce_scatter x1 -> x0, waiting for transfers between devices: 76.2 us -> none  [per_device(): lax.psum_scatter(partial_value.astype(jnp.bfloat16), 'tp', scatter_dimens...]
    all_gather x1 -> x2, waiting for transfers between devices: 73.7 us -> 2.28 us  [layer(): block_in = lax.all_gather(arrived, 'tp', axis=1, tiled=True)]
    ppermute x0 -> x9, waiting for transfers between devices: none -> 58.2 us  [shift(): lax.ppermute(value, 'tp', [(i, (i + by) % parts) for i in range(parts)])]
    pallas_call x0 -> x4, Pallas kernels: none -> 26.5 us  [the longest x2 13.4 us: down_of(): pl.pallas_call(down_kernel, grid=(steps,), in_specs=[pl.BlockSpec((rows,...]
    dot_general x3 -> x4, matrix products: 22.9 us -> 1.46 us  [the longest x2 0.88 us: layer(): jnp.dot(select, tokens, preferred_element_type=jnp.float32)]
    all_to_all x1 -> x2, waiting for transfers between devices: 45.2 us -> 24.9 us  [layer(): lax.all_to_all(out.reshape(experts, share, width), 'ep', split_axis=0, co...]
    ppermute x0 -> x9, starting transfers between devices: none -> 14.5 us  [shift(): lax.ppermute(value, 'tp', [(i, (i + by) % parts) for i in range(parts)])]
    all_to_all x1 -> x2, blocking collectives: 58.3 us -> 70.2 us  [layer(): lax.all_to_all(sending.reshape(experts, share, width), 'ep', split_axis=0...]
  transfers between devices with their start and end apart: 3 -> 13, of which waited for: 3 -> 9; matrix products, arithmetic and copies ran while one was open for 0% -> 5% of each run, Pallas kernels for 0% -> 11%
where the time goes in v1:
time: 251 us; the launch traced here: 250 us
  waiting for transfers between devices  85.4 us (34%)
  blocking collectives  70.2 us (28%)
  starting transfers between devices  36.2 us (14%)
  Pallas kernels  26.5 us (11%)
  local copies, waits for them, and re-layouts  14.8 us (6%)
  between operations  13.6 us (5%)
    all_to_all x2, blocking collectives, layer(): lax.all_to_all(sending.reshape(experts, share, width), 'ep', split_axis=0...  70.2 us
    ppermute x9, waiting for transfers between devices, shift(): lax.ppermute(value, 'tp', [(i, (i + by) % parts) for i in range(parts)])  58.2 us
    all_to_all x2, waiting for transfers between devices, layer(): lax.all_to_all(out.reshape(experts, share, width), 'ep', split_axis=0, co...  24.9 us
    all_to_all x2, starting transfers between devices, layer(): lax.all_to_all(out.reshape(experts, share, width), 'ep', split_axis=0, co...  21.7 us
    ppermute x9, starting transfers between devices, shift(): lax.ppermute(value, 'tp', [(i, (i + by) % parts) for i in range(parts)])  14.5 us
    pallas_call x2, Pallas kernels, down_of(): pl.pallas_call(down_kernel, grid=(steps,), in_specs=[pl.BlockSpec((rows,...  13.4 us
    pallas_call x2, Pallas kernels, hidden_of(): pl.pallas_call(hidden_kernel, grid=(steps,), in_specs=[pl.BlockSpec((rows...  13.1 us
    reshape x2, local copies, waits for them, and re-layouts, layer(): out.reshape(experts, share, width)  5.03 us
  transfers between devices with their start and end apart: 13, of which 9 were waited for; matrix products, arithmetic and copies ran while one was open for 5% of the time, Pallas kernels for 11%

profile of v1, /device:TPU:1, one launch (start us, length us, event | category | flops | bytes accessed | tf_op | source)
XLA Modules:
  0.0 250.1 jit_solution(2337438507981862308)
XLA Ops:
  6.5 0.8 copy.15
  9.5 38.5 %all_to_all.20 = bf16[64,4,1792]{2,1,0:T(4,128)(2,1)S(1)} all-to-all(bf16[64,4,1792]{2,1,0:T(4,128)(2,1)S(1)} %reshape.116), channel_id=1, replica_groups=mesh['ep'=64,'tp'=4] {'ep'}, dimensions={0} | all-to-all | bytes 1835008 | tf_op jit(solution)/shard_map/all_to_all | solution.py:113
  48.0 1.1 reshape.117
  49.9 31.7 %all_to_all.21 = bf16[64,4,1792]{2,1,0:T(4,128)(2,1)S(1)} all-to-all(bf16[64,4,1792]{2,1,0:T(4,128)(2,1)S(1)} %reshape.112), channel_id=1, replica_groups=mesh['ep'=64,'tp'=4] {'ep'}, dimensions={0} | all-to-all | bytes 1835008 | tf_op jit(solution)/shard_map/all_to_all | solution.py:113
  81.6 1.2 reshape.113
  82.9 4.0 %dynamic-slice_bitcast_fusion = (bf16[256,1792]{1,0:T(8,128)(2,1)}, bf16[256,1792]{1,0:T(8,128)(2,1)}, bf16[256,1792]{1,0:T(8,128)(2,1)}, bf16[256,1792]{1,0:T(8,128)(2,1)}) fusion(bf16[1,256,7168]{2,1,0:T(8,128)(2,1)} %param.11, s32[]{:T(128)S(6)} %select_n.80, s32[]{:T(128)S(6)} %select_n.78, s32[]{:T(128)S(6)} %select_n.77, s32[]{:T(128)S(6)} %select_n.79), kind=kLoop, calls=%fused_computation.2 | loop fusion | bytes 7340048 | tf_op jit(solution)/shard_map/dynamic_slice | solution.py:97
  86.9 2.7 %collective-permute-start.5 = (bf16[256,1792]{1,0:T(8,128)(2,1)}, bf16[256,1792]{1,0:T(8,128)(2,1)S(1)}, u32[]{:S(2)}, u32[]{:S(2)}) collective-permute-start(bf16[256,1792]{1,0:T(8,128)(2,1)} %get-tuple-element.13), channel_id=1, source_target_pairs={{0,3},{1,0},{2,1},{3,2},{4,7},{5,4},{6,5},{7,6},{8,11},{9,8},{10,9... | collective-permute-start | bytes 2752520 | tf_op jit(solution)/shard_map/ppermute | solution.py:92
  89.5 1.6 collective-permute-start.4
  91.2 2.3 all-gather.5.cloned.1.call-done.x_ref
  93.4 6.5 %hidden.3.refs_0_ = bf16[256,256]{1,0:T(8,128)(2,1)} custom-call(bf16[256,7168]{1,0:T(8,128)(2,1)} %all-gather.5.cloned.1.call-done.x_ref, bf16[1,7168,256]{2,1,0:T(8,128)(2,1)} %gate_ref.3, bf16[1,7168,256]{2,1,0:T(8,128)(2,1)} %up_ref.3), custom_call_target="tpu_custom_call" | custom-call | flops 1879048192 | bytes 11010048 | tf_op jit(solution)/shard_map/hidden/pallas_call | solution.py:34
  100.0 2.9 %collective-permute-start.7 = (bf16[256,256]{1,0:T(8,128)(2,1)}, bf16[256,256]{1,0:T(8,128)(2,1)S(1)}, u32[]{:S(2)}, u32[]{:S(2)}) collective-permute-start(bf16[256,256]{1,0:T(8,128)(2,1)} %hidden.3.refs_0_), channel_id=1, source_target_pairs={{0,2},{1,3},{2,0},{3,1},{4,6},{5,7},{6,4},{7,5},{8,10},{9,11},{10,... | collective-permute-start | bytes 393224 | tf_op jit(solution)/shard_map/ppermute | solution.py:92
  102.9 8.5 %collective-permute-done.5.refs_7_ = bf16[256,1792]{1,0:T(8,128)(2,1)S(1)} collective-permute-done((bf16[256,1792]{1,0:T(8,128)(2,1)}, bf16[256,1792]{1,0:T(8,128)(2,1)S(1)}, u32[]{:S(2)}, u32[]{:S(2)}) %collective-permute-start.5) | collective-permute-done | bytes 917536 | tf_op jit(solution)/shard_map/ppermute | solution.py:92
  111.5 1.2 collective-permute-start.6
  112.6 32.0 %collective-permute-done.4.refs_6_ = bf16[256,1792]{1,0:T(8,128)(2,1)S(1)} collective-permute-done((bf16[256,1792]{1,0:T(8,128)(2,1)}, bf16[256,1792]{1,0:T(8,128)(2,1)S(1)}, u32[]{:S(2)}, u32[]{:S(2)}) %collective-permute-start.4) | collective-permute-done | bytes 917536 | tf_op jit(solution)/shard_map/ppermute | solution.py:92
  144.7 5.8 %collective-permute-done.8.refs_3_ = bf16[256,256]{1,0:T(8,128)(2,1)S(1)} collective-permute-done((bf16[256,256]{1,0:T(8,128)(2,1)}, bf16[256,256]{1,0:T(8,128)(2,1)S(1)}, u32[]{:S(2)}, u32[]{:S(2)}) %collective-permute-start.8) | collective-permute-done | bytes 131104 | tf_op jit(solution)/shard_map/ppermute | solution.py:92
  150.5 3.4 %collective-permute-done.6.refs_1_ = bf16[256,256]{1,0:T(8,128)(2,1)S(1)} collective-permute-done((bf16[256,256]{1,0:T(8,128)(2,1)}, bf16[256,256]{1,0:T(8,128)(2,1)S(1)}, u32[]{:S(2)}, u32[]{:S(2)}) %collective-permute-start.6) | collective-permute-done | bytes 131104 | tf_op jit(solution)/shard_map/ppermute | solution.py:92
  153.9 0.6 copy-done.7
  154.5 6.7 %down.3 = bf16[256,1792]{1,0:T(8,128)(2,1)} custom-call(bf16[256,256]{1,0:T(8,128)(2,1)} %hidden.3.refs_0_, bf16[256,256]{1,0:T(8,128)(2,1)} %copy-done.7, bf16[256,256]{1,0:T(8,128)(2,1)} %copy-done.5, bf16[256,256]{1,0:T(8,128)(2,1)} %copy-done.4, bf16[256,1792]{1,0:T(8,128)(2,1)} %get-tuple-element.15.refs_4_, bf16[256,1792]{1,0:T(8,128)(2,1)} %copy-done.2, ...), custom_call_target="tpu_custom_call" | custom-call | flops 939524096 | bytes 5111808 | tf_op jit(solution)/shard_map/down/pallas_call | solution.py:65
  161.2 2.5 %reshape.118 = bf16[64,4,1792]{2,1,0:T(4,128)(2,1)} reshape(bf16[256,1792]{1,0:T(8,128)(2,1)} %down.3) | data formatting | bytes 1835008 | tf_op jit(solution)/shard_map/reshape | solution.py:122
  163.8 10.9 %all-to-all-start.3 = ((bf16[64,4,1792]{2,1,0:T(4,128)(2,1)}), bf16[64,4,1792]{2,1,0:T(4,128)(2,1)S(1)}, u32[]{:S(2)}, u32[]{:S(2)}) async-start(bf16[64,4,1792]{2,1,0:T(4,128)(2,1)} %reshape.118), calls=%async_computation.3 | async-start | bytes 1835008 | tf_op jit(solution)/shard_map/all_to_all | solution.py:121
  174.7 6.6 %hidden.2.refs_0_ = bf16[256,256]{1,0:T(8,128)(2,1)} custom-call(bf16[256,7168]{1,0:T(8,128)(2,1)} %all-gather.3.cloned.1.call-done.x_ref, bf16[1,7168,256]{2,1,0:T(8,128)(2,1)} %gate_ref.3, bf16[1,7168,256]{2,1,0:T(8,128)(2,1)} %up_ref.3), custom_call_target="tpu_custom_call" | custom-call | flops 1879048192 | bytes 11010048 | tf_op jit(solution)/shard_map/hidden/pallas_call | solution.py:34
  181.3 4.8 %collective-permute-start.2 = (bf16[256,256]{1,0:T(8,128)(2,1)}, bf16[256,256]{1,0:T(8,128)(2,1)S(1)}, u32[]{:S(2)}, u32[]{:S(2)}) collective-permute-start(bf16[256,256]{1,0:T(8,128)(2,1)} %hidden.2.refs_0_), channel_id=1, source_target_pairs={{0,3},{1,0},{2,1},{3,2},{4,7},{5,4},{6,5},{7,6},{8,11},{9,8},{10,9... | collective-permute-start | bytes 393224 | tf_op jit(solution)/shard_map/ppermute | solution.py:92
  186.1 1.2 collective-permute-start.1
  187.3 1.8 collective-permute-done.2.refs_3_
  189.2 3.0 %collective-permute-done.1.refs_2_ = bf16[256,256]{1,0:T(8,128)(2,1)S(1)} collective-permute-done((bf16[256,256]{1,0:T(8,128)(2,1)}, bf16[256,256]{1,0:T(8,128)(2,1)S(1)}, u32[]{:S(2)}, u32[]{:S(2)}) %collective-permute-start.1) | collective-permute-done | bytes 131104 | tf_op jit(solution)/shard_map/ppermute | solution.py:92
  192.2 3.6 %collective-permute-done.refs_1_ = bf16[256,256]{1,0:T(8,128)(2,1)S(1)} collective-permute-done((bf16[256,256]{1,0:T(8,128)(2,1)}, bf16[256,256]{1,0:T(8,128)(2,1)S(1)}, u32[]{:S(2)}, u32[]{:S(2)}) %collective-permute-start) | collective-permute-done | bytes 131104 | tf_op jit(solution)/shard_map/ppermute | solution.py:92
  195.8 0.6 copy-done.9
  196.4 6.7 %down.2 = bf16[256,1792]{1,0:T(8,128)(2,1)} custom-call(bf16[256,256]{1,0:T(8,128)(2,1)} %hidden.2.refs_0_, bf16[256,256]{1,0:T(8,128)(2,1)} %copy-done.9, bf16[256,256]{1,0:T(8,128)(2,1)} %copy-done.8, bf16[256,256]{1,0:T(8,128)(2,1)} %copy-done.6, bf16[256,1792]{1,0:T(8,128)(2,1)} %get-tuple-element.15.refs_4_, bf16[256,1792]{1,0:T(8,128)(2,1)} %copy-done.2, ...), custom_call_target="tpu_custom_call" | custom-call | flops 939524096 | bytes 5111808 | tf_op jit(solution)/shard_map/down/pallas_call | solution.py:65
  203.1 2.5 %reshape.114 = bf16[64,4,1792]{2,1,0:T(4,128)(2,1)} reshape(bf16[256,1792]{1,0:T(8,128)(2,1)} %down.2) | data formatting | bytes 1835008 | tf_op jit(solution)/shard_map/reshape | solution.py:122
  205.6 10.7 %all-to-all-start.1 = ((bf16[64,4,1792]{2,1,0:T(4,128)(2,1)}), bf16[64,4,1792]{2,1,0:T(4,128)(2,1)S(1)}, u32[]{:S(2)}, u32[]{:S(2)}) async-start(bf16[64,4,1792]{2,1,0:T(4,128)(2,1)} %reshape.114), calls=%async_computation.1 | async-start | bytes 1835008 | tf_op jit(solution)/shard_map/all_to_all | solution.py:121
  217.2 24.9 %all-to-all-done.1 = bf16[64,4,1792]{2,1,0:T(4,128)(2,1)S(1)} async-done(((bf16[64,4,1792]{2,1,0:T(4,128)(2,1)}), bf16[64,4,1792]{2,1,0:T(4,128)(2,1)S(1)}, u32[]{:S(2)}, u32[]{:S(2)}) %all-to-all-start.1) | async-done | bytes 917536 | tf_op jit(solution)/shard_map/all_to_all | solution.py:121
  242.6 0.7 fusion.1
  (55 shorter events, 4.2 us)
Async XLA Ops:
  6.5 2.3 copy-start
  6.5 86.9 %all-gather.5.cloned.1.call-start = ((), (), s32[]{:S(2)}) async-start(), calls=%async_computation.5 | async-start | bytes 4587520 | tf_op jit(solution)/shard_map/all_gather | solution.py:117
  49.2 125.6 %all-gather.3.cloned.1.call-start = ((), (), s32[]{:S(2)}) async-start(), calls=%async_computation.4 | async-start | bytes 4587520 | tf_op jit(solution)/shard_map/all_gather | solution.py:117
  86.9 24.6 %collective-permute-start.5 = (bf16[256,1792]{1,0:T(8,128)(2,1)}, bf16[256,1792]{1,0:T(8,128)(2,1)S(1)}, u32[]{:S(2)}, u32[]{:S(2)}) collective-permute-start(bf16[256,1792]{1,0:T(8,128)(2,1)} %get-tuple-element.13), channel_id=1, source_target_pairs={{0,3},{1,0},{2,1},{3,2},{4,7},{5,4},{6,5},{7,6},{8,11},{9,8},{10,9... | collective-permute-start | bytes 2752520 | tf_op jit(solution)/shard_map/ppermute | solution.py:92
  89.5 23.1 %collective-permute-start.3 = (bf16[256,1792]{1,0:T(8,128)(2,1)}, bf16[256,1792]{1,0:T(8,128)(2,1)S(1)}, u32[]{:S(2)}, u32[]{:S(2)}) collective-permute-start(bf16[256,1792]{1,0:T(8,128)(2,1)} %get-tuple-element.14), channel_id=1, source_target_pairs={{0,1},{1,2},{2,3},{3,0},{4,5},{5,6},{6,7},{7,4},{8,9},{9,10},{10,1... | collective-permute-start | bytes 2752520 | tf_op jit(solution)/shard_map/ppermute | solution.py:92
  89.5 55.2 %collective-permute-start.4 = (bf16[256,1792]{1,0:T(8,128)(2,1)}, bf16[256,1792]{1,0:T(8,128)(2,1)S(1)}, u32[]{:S(2)}, u32[]{:S(2)}) collective-permute-start(bf16[256,1792]{1,0:T(8,128)(2,1)} %get-tuple-element.16), channel_id=1, source_target_pairs={{0,2},{1,3},{2,0},{3,1},{4,6},{5,7},{6,4},{7,5},{8,10},{9,11},{10,... | collective-permute-start | bytes 2752520 | tf_op jit(solution)/shard_map/ppermute | solution.py:92
  100.0 50.5 %collective-permute-start.8 = (bf16[256,256]{1,0:T(8,128)(2,1)}, bf16[256,256]{1,0:T(8,128)(2,1)S(1)}, u32[]{:S(2)}, u32[]{:S(2)}) collective-permute-start(bf16[256,256]{1,0:T(8,128)(2,1)} %hidden.3.refs_0_), channel_id=1, source_target_pairs={{0,3},{1,0},{2,1},{3,2},{4,7},{5,4},{6,5},{7,6},{8,11},{9,8},{10,9... | collective-permute-start | bytes 393224 | tf_op jit(solution)/shard_map/ppermute | solution.py:92
  100.0 50.5 %collective-permute-start.7 = (bf16[256,256]{1,0:T(8,128)(2,1)}, bf16[256,256]{1,0:T(8,128)(2,1)S(1)}, u32[]{:S(2)}, u32[]{:S(2)}) collective-permute-start(bf16[256,256]{1,0:T(8,128)(2,1)} %hidden.3.refs_0_), channel_id=1, source_target_pairs={{0,2},{1,3},{2,0},{3,1},{4,6},{5,7},{6,4},{7,5},{8,10},{9,11},{10,... | collective-permute-start | bytes 393224 | tf_op jit(solution)/shard_map/ppermute | solution.py:92
  111.5 42.4 %copy-start.1 = (bf16[256,1792]{1,0:T(8,128)(2,1)}, bf16[256,1792]{1,0:T(8,128)(2,1)S(1)}, u32[]{:S(2)}) copy-start(bf16[256,1792]{1,0:T(8,128)(2,1)S(1)} %collective-permute-done.5.refs_7_) | copy-start | bytes 2752516
  111.5 42.4 %collective-permute-start.6 = (bf16[256,256]{1,0:T(8,128)(2,1)}, bf16[256,256]{1,0:T(8,128)(2,1)S(1)}, u32[]{:S(2)}, u32[]{:S(2)}) collective-permute-start(bf16[256,256]{1,0:T(8,128)(2,1)} %hidden.3.refs_0_), channel_id=1, source_target_pairs={{0,1},{1,2},{2,3},{3,0},{4,5},{5,6},{6,7},{7,4},{8,9},{9,10},{10,1... | collective-permute-start | bytes 393224 | tf_op jit(solution)/shard_map/ppermute | solution.py:92
  112.6 41.2 %copy-start.2 = (bf16[256,1792]{1,0:T(8,128)(2,1)}, bf16[256,1792]{1,0:T(8,128)(2,1)S(1)}, u32[]{:S(2)}) copy-start(bf16[256,1792]{1,0:T(8,128)(2,1)S(1)} %collective-permute-done.3.refs_5_) | copy-start | bytes 2752516
  144.7 9.2 %copy-start.3 = (bf16[256,1792]{1,0:T(8,128)(2,1)}, bf16[256,1792]{1,0:T(8,128)(2,1)S(1)}, u32[]{:S(2)}) copy-start(bf16[256,1792]{1,0:T(8,128)(2,1)S(1)} %collective-permute-done.4.refs_6_) | copy-start | bytes 2752516
  150.5 3.4 %copy-start.4 = (bf16[256,256]{1,0:T(8,128)(2,1)}, bf16[256,256]{1,0:T(8,128)(2,1)S(1)}, u32[]{:S(2)}) copy-start(bf16[256,256]{1,0:T(8,128)(2,1)S(1)} %collective-permute-done.8.refs_3_) | copy-start | bytes 393220
  150.5 3.4 %copy-start.5 = (bf16[256,256]{1,0:T(8,128)(2,1)}, bf16[256,256]{1,0:T(8,128)(2,1)S(1)}, u32[]{:S(2)}) copy-start(bf16[256,256]{1,0:T(8,128)(2,1)S(1)} %collective-permute-done.7.refs_2_) | copy-start | bytes 393220
  153.9 0.7 copy-start.7
  163.8 41.9 %all-to-all-start.3 = ((bf16[64,4,1792]{2,1,0:T(4,128)(2,1)}), bf16[64,4,1792]{2,1,0:T(4,128)(2,1)S(1)}, u32[]{:S(2)}, u32[]{:S(2)}) async-start(bf16[64,4,1792]{2,1,0:T(4,128)(2,1)} %reshape.118), calls=%async_computation.3 | async-start | bytes 1835008 | tf_op jit(solution)/shard_map/all_to_all | solution.py:121
  181.3 35.1 %copy-start.10 = (f32[32,8]{0,1:T(8,128)S(1)}, f32[32,8]{0,1:T(8,128)}, u32[]{:S(2)}) copy-start(f32[32,8]{0,1:T(8,128)} %param.8) | copy-start | bytes 3076
  181.3 7.9 %collective-permute-start.2 = (bf16[256,256]{1,0:T(8,128)(2,1)}, bf16[256,256]{1,0:T(8,128)(2,1)S(1)}, u32[]{:S(2)}, u32[]{:S(2)}) collective-permute-start(bf16[256,256]{1,0:T(8,128)(2,1)} %hidden.2.refs_0_), channel_id=1, source_target_pairs={{0,3},{1,0},{2,1},{3,2},{4,7},{5,4},{6,5},{7,6},{8,11},{9,8},{10,9... | collective-permute-start | bytes 393224 | tf_op jit(solution)/shard_map/ppermute | solution.py:92
  186.1 6.0 %collective-permute-start.1 = (bf16[256,256]{1,0:T(8,128)(2,1)}, bf16[256,256]{1,0:T(8,128)(2,1)S(1)}, u32[]{:S(2)}, u32[]{:S(2)}) collective-permute-start(bf16[256,256]{1,0:T(8,128)(2,1)} %hidden.2.refs_0_), channel_id=1, source_target_pairs={{0,2},{1,3},{2,0},{3,1},{4,6},{5,7},{6,4},{7,5},{8,10},{9,11},{10,... | collective-permute-start | bytes 393224 | tf_op jit(solution)/shard_map/ppermute | solution.py:92
  187.3 8.4 %collective-permute-start = (bf16[256,256]{1,0:T(8,128)(2,1)}, bf16[256,256]{1,0:T(8,128)(2,1)S(1)}, u32[]{:S(2)}, u32[]{:S(2)}) collective-permute-start(bf16[256,256]{1,0:T(8,128)(2,1)} %hidden.2.refs_0_), channel_id=1, source_target_pairs={{0,1},{1,2},{2,3},{3,0},{4,5},{5,6},{6,7},{7,4},{8,9},{9,10},{10,1... | collective-permute-start | bytes 393224 | tf_op jit(solution)/shard_map/ppermute | solution.py:92
  189.2 6.6 %copy-start.6 = (bf16[256,256]{1,0:T(8,128)(2,1)}, bf16[256,256]{1,0:T(8,128)(2,1)S(1)}, u32[]{:S(2)}) copy-start(bf16[256,256]{1,0:T(8,128)(2,1)S(1)} %collective-permute-done.2.refs_3_) | copy-start | bytes 393220
  192.2 3.6 %copy-start.8 = (bf16[256,256]{1,0:T(8,128)(2,1)}, bf16[256,256]{1,0:T(8,128)(2,1)S(1)}, u32[]{:S(2)}) copy-start(bf16[256,256]{1,0:T(8,128)(2,1)S(1)} %collective-permute-done.1.refs_2_) | copy-start | bytes 393220
  195.8 0.6 copy-start.9
  205.6 36.4 %all-to-all-start.1 = ((bf16[64,4,1792]{2,1,0:T(4,128)(2,1)}), bf16[64,4,1792]{2,1,0:T(4,128)(2,1)S(1)}, u32[]{:S(2)}, u32[]{:S(2)}) async-start(bf16[64,4,1792]{2,1,0:T(4,128)(2,1)} %reshape.114), calls=%async_computation.1 | async-start | bytes 1835008 | tf_op jit(solution)/shard_map/all_to_all | solution.py:121
Sparse Core Ops, SparseCore 0:
  49.3 44.0 all-gather.4
  95.2 73.0 all-gather.2

commit v2 on v1

v2 whole, which is shorter than its diff:
```python
import functools

import jax
import jax.numpy as jnp
from jax import lax
from jax.experimental import pallas as pl
from jax.experimental.pallas import tpu as pltpu
from jax.sharding import PartitionSpec as P


SIZES = (4, 4)
TILE = 256
F32 = jnp.float32
BF16 = jnp.bfloat16


def vmem():
    return pl.BlockSpec(memory_space=pltpu.VMEM)


def hidden_kernel(order_ref, mine, left, right, front, rear, gate_ref, up_ref, out_ref, gate_acc, up_acc):
    step = pl.program_id(0)

    def add(block, rows):
        gate_acc[rows, :] += jnp.dot(block[...], gate_ref[...], preferred_element_type=F32)
        up_acc[rows, :] += jnp.dot(block[...], up_ref[...], preferred_element_type=F32)

    rows = mine.shape[0] // 2
    lower, upper = pl.ds(0, rows), pl.ds(rows, rows)

    @pl.when(step == 0)
    def _():
        gate_acc[...] = jnp.zeros_like(gate_acc)
        up_acc[...] = jnp.zeros_like(up_acc)

    for i, block in enumerate((mine, left, right)):

        @pl.when(step == i)
        def _(block=block):
            add(block, slice(None))

    @pl.when(step == 3)
    def _():
        add(front, lower)
        add(rear, upper)
        gate = gate_acc[...]
        out_ref[...] = (gate / (1.0 + jnp.exp(-gate)) * up_acc[...]).astype(BF16)


def hidden_of(order, blocks, gate_proj, up_proj):
    rows, depth = blocks[0].shape
    cols = gate_proj.shape[2]
    weight = pl.BlockSpec((None, depth, cols), lambda k, order: (0, order[k], 0))
    return pl.pallas_call(
        hidden_kernel,
        grid_spec=pltpu.PrefetchScalarGridSpec(
            num_scalar_prefetch=1,
            grid=(4,),
            in_specs=[pl.BlockSpec(b.shape, lambda k, order: (0, 0)) for b in blocks] + [weight, weight],
            out_specs=pl.BlockSpec((rows, cols), lambda k, order: (0, 0)),
            scratch_shapes=[pltpu.VMEM((rows, cols), F32)] * 2,
        ),
        out_shape=jax.ShapeDtypeStruct((rows, cols), BF16),
        cost_estimate=pl.CostEstimate(
            flops=16 * rows * depth * cols,
            bytes_accessed=8 * depth * (rows + 2 * cols),
            transcendentals=rows * cols,
        ),
        name="hidden",
    )(order, *blocks, gate_proj, up_proj)


def down_kernel(pairs, *refs):
    out = refs[-1]
    hidden = jnp.concatenate([r[...] for r in refs[:pairs]], axis=1)

    @pl.loop(0, out.shape[1] // TILE)
    def _(k):
        at = pl.ds(pl.multiple_of(k * TILE, TILE), TILE)
        weight = jnp.concatenate([r[:, at] for r in refs[pairs : 2 * pairs]])
        out[:, at] = jnp.dot(hidden, weight, preferred_element_type=F32).astype(BF16)


def down_of(hiddens, downs):
    rows, inner = hiddens[0].shape
    width = downs[0].shape[1]
    n = len(hiddens)
    return pl.pallas_call(
        functools.partial(down_kernel, n),
        in_specs=[vmem()] * (2 * n),
        out_specs=vmem(),
        out_shape=jax.ShapeDtypeStruct((rows, width), BF16),
        cost_estimate=pl.CostEstimate(
            flops=2 * n * rows * inner * width,
            bytes_accessed=2 * n * inner * (rows + width) + 2 * rows * width,
            transcendentals=0,
        ),
        name="down",
    )(*hiddens, *downs)


def layer(tokens, routes, route_weights, gate_proj, up_proj, down_proj):
    w_down = down_proj[0]
    tok_count, width = tokens.shape
    fanout = routes.shape[1]
    experts = lax.axis_size("ep")
    parts = lax.axis_size("tp")
    tp = lax.axis_index("tp")
    capacity = sum(SIZES)
    order = (tp + jnp.array([0, parts - 1, 1, 2], jnp.int32)) % parts

    def over_y(value, by):
        return lax.ppermute(value, "tp", [(i, (i + by) % parts) for i in range(parts)])

    def exchange(value):
        blocks = value.reshape(experts, value.shape[0] // experts, width)
        blocks = lax.all_to_all(blocks, "ep", split_axis=0, concat_axis=0, tiled=True)
        return blocks.reshape(value.shape)

    downs = []
    for by in range(parts):
        start = (tp + by) % parts * width
        piece = lax.dynamic_slice_in_dim(w_down, start, width, axis=1)
        downs.append(piece if by == 0 else over_y(piece, by))

    flat_ids = routes.reshape(-1)
    onehot = (flat_ids[:, None] == jnp.arange(experts, dtype=jnp.int32)[None, :]).astype(jnp.int32)
    before = jnp.cumsum(onehot, axis=0) - onehot
    position = jnp.sum(before * onehot, axis=1)
    target = (flat_ids * capacity + position).reshape(tok_count, fanout)

    mixed = jnp.zeros((tok_count, width), F32)
    first = 0
    for size in SIZES:
        row = jnp.arange(experts * size, dtype=jnp.int32)
        slot = row // size * capacity + first + row % size
        first += size
        select = jnp.any(target[None, :, :] == slot[:, None, None], axis=2).astype(BF16)
        sending = jnp.dot(select, tokens, preferred_element_type=F32).astype(BF16)
        mine = exchange(sending)
        cut = mine.shape[0] // 2
        left = over_y(mine, 1)
        right = over_y(mine, -1)
        front = over_y(left[:cut], 1)
        rear = over_y(right[cut:], -1)
        hidden = hidden_of(order, [mine, left, right, front, rear], gate_proj, up_proj)
        hiddens = [hidden] + [over_y(hidden, by) for by in range(1, parts)]
        out = down_of(hiddens, downs)
        back = exchange(out)
        weight = jnp.sum(
            jnp.where(target[:, :, None] == slot[None, None, :], route_weights[:, :, None], 0.0), axis=1
        )
        high = lax.reduce_precision(weight, 8, 7)
        both = jnp.concatenate([high, weight - high]).astype(BF16)
        both = jnp.dot(both, back, preferred_element_type=F32)
        mixed = mixed + (both[:tok_count] + both[tok_count:])
    return mixed.astype(BF16)


def solution(mesh):
    in_specs = (
        P("ep", "tp"),
        P("ep", None),
        P("ep", None),
        P("ep", None, "tp"),
        P("ep", None, "tp"),
        P("ep", "tp", None),
    )
    out_specs = P("ep", "tp")
    return jax.shard_map(layer, mesh=mesh, in_specs=in_specs, out_specs=out_specs, check_vma=False)
```

time: 251 us -> 265 us (1.056)
  blocking collectives: 70.2 us -> 0 us
  waiting for transfers between devices: 85.4 us -> 153 us
  starting transfers between devices: 36.2 us -> 61.3 us
  between operations: 13.6 us -> 0.26 us
  local copies, waits for them, and re-layouts: 14.8 us -> 20.2 us
    all_to_all x2 -> x0, blocking collectives: 70.2 us -> none  [layer(): lax.all_to_all(sending.reshape(experts, share, width), 'ep', split_axis=0...]
    ppermute x9 -> x17, waiting for transfers between devices: 58.2 us -> 104 us  [over_y(): lax.ppermute(value, 'tp', [(i, (i + by) % parts) for i in range(parts)])]
    all_to_all x2 -> x4, waiting for transfers between devices: 24.9 us -> 49 us  [exchange(): lax.all_to_all(blocks, 'ep', split_axis=0, concat_axis=0, tiled=True)]
    all_to_all x2 -> x4, starting transfers between devices: 21.7 us -> 44.8 us  [exchange(): lax.all_to_all(blocks, 'ep', split_axis=0, concat_axis=0, tiled=True)]
    ppermute x9 -> x17, starting transfers between devices: 14.5 us -> 16.5 us  [over_y(): lax.ppermute(value, 'tp', [(i, (i + by) % parts) for i in range(parts)])]
  transfers between devices with their start and end apart: 13 -> 21, of which waited for: 9 -> 14; matrix products, arithmetic and copies ran while one was open for 5% -> 6% of each run, Pallas kernels for 11% -> 10%
where the time goes in v2:
time: 265 us; the launch traced here: 264 us
  waiting for transfers between devices  153 us (58%)
  starting transfers between devices  61.3 us (23%)
  Pallas kernels  25.8 us (10%)
  local copies, waits for them, and re-layouts  20.2 us (8%)
    ppermute x17, waiting for transfers between devices, over_y(): lax.ppermute(value, 'tp', [(i, (i + by) % parts) for i in range(parts)])  104 us
    all_to_all x4, waiting for transfers between devices, exchange(): lax.all_to_all(blocks, 'ep', split_axis=0, concat_axis=0, tiled=True)  49 us
    all_to_all x4, starting transfers between devices, exchange(): lax.all_to_all(blocks, 'ep', split_axis=0, concat_axis=0, tiled=True)  44.8 us
    ppermute x17, starting transfers between devices, over_y(): lax.ppermute(value, 'tp', [(i, (i + by) % parts) for i in range(parts)])  16.5 us
    pallas_call x2, Pallas kernels, hidden_of(): pl.pallas_call(hidden_kernel, grid_spec=pltpu.PrefetchScalarGridSpec(num_...  15 us
    pallas_call x2, Pallas kernels, down_of(): pl.pallas_call(functools.partial(down_kernel, n), in_specs=[vmem()] * (2...  10.7 us
    reshape x4, local copies, waits for them, and re-layouts, exchange(): blocks = value.reshape(experts, value.shape[0] // experts, width)  7.37 us
  transfers between devices with their start and end apart: 21, of which 14 were waited for; matrix products, arithmetic and copies ran while one was open for 6% of the time, Pallas kernels for 10%

profile of v2, /device:TPU:1, one launch (start us, length us, event | category | flops | bytes accessed | tf_op | source)
XLA Modules:
  0.0 264.1 jit_solution(2156785885387745705)
XLA Ops:
  3.9 13.0 %all-to-all-start.2 = ((bf16[64,4,1792]{2,1,0:T(4,128)(2,1)}), bf16[64,4,1792]{2,1,0:T(4,128)(2,1)S(1)}, u32[]{:S(2)}, u32[]{:S(2)}) async-start(bf16[64,4,1792]{2,1,0:T(4,128)(2,1)} %reshape.116), calls=%async_computation.2 | async-start | bytes 1835008 | tf_op jit(solution)/shard_map/all_to_all | solution.py:117
  17.3 1.2 reshape.112
  18.5 24.1 %all-to-all-done.2 = bf16[64,4,1792]{2,1,0:T(4,128)(2,1)S(1)} async-done(((bf16[64,4,1792]{2,1,0:T(4,128)(2,1)}), bf16[64,4,1792]{2,1,0:T(4,128)(2,1)S(1)}, u32[]{:S(2)}, u32[]{:S(2)}) %all-to-all-start.2) | async-done | bytes 917536 | tf_op jit(solution)/shard_map/all_to_all | solution.py:117
  42.6 6.4 %all-to-all-start = ((bf16[64,4,1792]{2,1,0:T(4,128)(2,1)}), bf16[64,4,1792]{2,1,0:T(4,128)(2,1)}, u32[]{:S(2)}, u32[]{:S(2)}) async-start(bf16[64,4,1792]{2,1,0:T(4,128)(2,1)} %reshape.112), calls=%async_computation | async-start | bytes 1835008 | tf_op jit(solution)/shard_map/all_to_all | solution.py:117
  50.2 2.7 %collective-permute-start.11 = (bf16[256,1792]{1,0:T(8,128)(2,1)}, bf16[256,1792]{1,0:T(8,128)(2,1)}, u32[]{:S(2)}, u32[]{:S(2)}) collective-permute-start(bf16[256,1792]{1,0:T(8,128)(2,1)} %reshape.117.mine), channel_id=1, source_target_pairs={{0,3},{1,0},{2,1},{3,2},{4,7},{5,4},{6,5},{7,6},{8,11},{9,8},{10,9... | collective-permute-start | bytes 2752520 | tf_op jit(solution)/shard_map/ppermute | solution.py:113
  52.9 3.9 %dynamic-slice_bitcast_fusion = (bf16[256,1792]{1,0:T(8,128)(2,1)}, bf16[256,1792]{1,0:T(8,128)(2,1)}, bf16[256,1792]{1,0:T(8,128)(2,1)}, bf16[256,1792]{1,0:T(8,128)(2,1)}) fusion(bf16[1,256,7168]{2,1,0:T(8,128)(2,1)} %param.12, s32[]{:T(128)S(6)} %select_n.109, s32[]{:T(128)S(6)} %select_n.105, s32[]{:T(128)S(6)} %select_n.103, s32[]{:T(128)S(6)} %select_n.107), kind=kLoop, calls=%fused_computation.2 | loop fusion | bytes 7340048 | tf_op jit(solution)/shard_map/dynamic_slice | solution.py:123
  56.8 2.7 %collective-permute-start.9 = (bf16[256,1792]{1,0:T(8,128)(2,1)}, bf16[256,1792]{1,0:T(8,128)(2,1)S(1)}, u32[]{:S(2)}, u32[]{:S(2)}) collective-permute-start(bf16[256,1792]{1,0:T(8,128)(2,1)} %get-tuple-element.9), channel_id=1, source_target_pairs={{0,3},{1,0},{2,1},{3,2},{4,7},{5,4},{6,5},{7,6},{8,11},{9,8},{10,9... | collective-permute-start | bytes 2752520 | tf_op jit(solution)/shard_map/ppermute | solution.py:113
  59.5 1.2 collective-permute-start.8
  60.6 11.7 %collective-permute-done.11.right = bf16[256,1792]{1,0:T(8,128)(2,1)} collective-permute-done((bf16[256,1792]{1,0:T(8,128)(2,1)}, bf16[256,1792]{1,0:T(8,128)(2,1)}, u32[]{:S(2)}, u32[]{:S(2)}) %collective-permute-start.11) | collective-permute-done | bytes 917536 | tf_op jit(solution)/shard_map/ppermute | solution.py:113
  73.4 3.5 %collective-permute-start.13 = (bf16[128,1792]{1,0:T(8,128)(2,1)S(1)}, bf16[128,1792]{1,0:T(8,128)(2,1)S(1)}, u32[]{:S(2)}, u32[]{:S(2)}) collective-permute-start(bf16[128,1792]{1,0:T(8,128)(2,1)S(1)} %slice.46), channel_id=1, source_target_pairs={{0,3},{1,0},{2,1},{3,2},{4,7},{5,4},{6,5},{7,6},{8,11},{9,8},{10,9... | collective-permute-start | bytes 1376264 | tf_op jit(solution)/shard_map/ppermute | solution.py:113
  78.6 42.8 %collective-permute-done.13.rear = bf16[128,1792]{1,0:T(8,128)(2,1)S(1)} collective-permute-done((bf16[128,1792]{1,0:T(8,128)(2,1)S(1)}, bf16[128,1792]{1,0:T(8,128)(2,1)S(1)}, u32[]{:S(2)}, u32[]{:S(2)}) %collective-permute-start.13) | collective-permute-done | bytes 458784 | tf_op jit(solution)/shard_map/ppermute | solution.py:113
  121.4 3.2 %collective-permute-done.12.front = bf16[128,1792]{1,0:T(8,128)(2,1)} collective-permute-done((bf16[128,1792]{1,0:T(8,128)(2,1)S(1)}, bf16[128,1792]{1,0:T(8,128)(2,1)}, u32[]{:S(2)}, u32[]{:S(2)}) %collective-permute-start.12) | collective-permute-done | bytes 458784 | tf_op jit(solution)/shard_map/ppermute | solution.py:113
  124.7 7.5 %hidden.3.refs_0_ = bf16[256,256]{1,0:T(8,128)(2,1)} custom-call(s32[4]{0:T(128)} %and_select_fusion.order_ref, bf16[256,1792]{1,0:T(8,128)(2,1)} %reshape.117.mine, bf16[256,1792]{1,0:T(8,128)(2,1)} %collective-permute-done.10.left, bf16[256,1792]{1,0:T(8,128)(2,1)} %collective-permute-done.11.right, bf16[128,1792]{1,0:T(8,128)(2,1)} %collective-permute-done.12.front, ...), custom_call_target="tpu_custom_call" | custom-call | flops 1879048192 | bytes 11010048 | tf_op jit(solution)/shard_map/hidden/pallas_call | solution.py:54
  133.8 2.4 collective-permute-done.16.refs_3_
  136.2 2.6 collective-permute-done.15.refs_2_
  138.8 3.5 %collective-permute-done.14.refs_1_ = bf16[256,256]{1,0:T(8,128)(2,1)S(1)} collective-permute-done((bf16[256,256]{1,0:T(8,128)(2,1)}, bf16[256,256]{1,0:T(8,128)(2,1)S(1)}, u32[]{:S(2)}, u32[]{:S(2)}) %collective-permute-start.14) | collective-permute-done | bytes 131104 | tf_op jit(solution)/shard_map/ppermute | solution.py:113
  143.0 5.3 %down.3 = bf16[256,1792]{1,0:T(8,128)(2,1)} custom-call(bf16[256,256]{1,0:T(8,128)(2,1)} %hidden.3.refs_0_, bf16[256,256]{1,0:T(8,128)(2,1)} %copy-done.12, bf16[256,256]{1,0:T(8,128)(2,1)} %copy-done.10, bf16[256,256]{1,0:T(8,128)(2,1)} %copy-done.9, bf16[256,1792]{1,0:T(8,128)(2,1)} %get-tuple-element.11.refs_4_, bf16[256,1792]{1,0:T(8,128)(2,1)} %copy-done.2, ...), custom_call_target="tpu_custom_call" | custom-call | flops 939524096 | bytes 5111808 | tf_op jit(solution)/shard_map/down/pallas_call | solution.py:88
  148.3 2.5 reshape.118
  150.8 11.3 %all-to-all-start.3 = ((bf16[64,4,1792]{2,1,0:T(4,128)(2,1)}), bf16[64,4,1792]{2,1,0:T(4,128)(2,1)S(1)}, u32[]{:S(2)}, u32[]{:S(2)}) async-start(bf16[64,4,1792]{2,1,0:T(4,128)(2,1)} %reshape.118), calls=%async_computation.3 | async-start | bytes 1835008 | tf_op jit(solution)/shard_map/all_to_all | solution.py:117
  162.2 1.7 reshape.113.mine
  165.4 20.0 %collective-permute-done.1.right = bf16[256,1792]{1,0:T(8,128)(2,1)S(1)} collective-permute-done((bf16[256,1792]{1,0:T(8,128)(2,1)S(1)}, bf16[256,1792]{1,0:T(8,128)(2,1)S(1)}, u32[]{:S(2)}, u32[]{:S(2)}) %collective-permute-start.1) | collective-permute-done | bytes 917536 | tf_op jit(solution)/shard_map/ppermute | solution.py:113
  185.4 1.7 collective-permute-start.3
  188.1 8.2 %collective-permute-done.3.rear = bf16[128,1792]{1,0:T(8,128)(2,1)S(1)} collective-permute-done((bf16[128,1792]{1,0:T(8,128)(2,1)S(1)}, bf16[128,1792]{1,0:T(8,128)(2,1)S(1)}, u32[]{:S(2)}, u32[]{:S(2)}) %collective-permute-start.3) | collective-permute-done | bytes 458784 | tf_op jit(solution)/shard_map/ppermute | solution.py:113
  196.3 3.6 %collective-permute-done.2.front = bf16[128,1792]{1,0:T(8,128)(2,1)} collective-permute-done((bf16[128,1792]{1,0:T(8,128)(2,1)S(1)}, bf16[128,1792]{1,0:T(8,128)(2,1)}, u32[]{:S(2)}, u32[]{:S(2)}) %collective-permute-start.2) | collective-permute-done | bytes 458784 | tf_op jit(solution)/shard_map/ppermute | solution.py:113
  199.9 7.5 %hidden.2.refs_0_ = bf16[256,256]{1,0:T(8,128)(2,1)} custom-call(s32[4]{0:T(128)} %and_select_fusion.order_ref, bf16[256,1792]{1,0:T(8,128)(2,1)} %copy-done.4, bf16[256,1792]{1,0:T(8,128)(2,1)} %copy-done.6, bf16[256,1792]{1,0:T(8,128)(2,1)} %copy-done.5, bf16[128,1792]{1,0:T(8,128)(2,1)} %collective-permute-done.2.front, bf16[128,1792]{1,0:T(8,128)(2,1)} %copy-done.8, ...), custom_call_target="tpu_custom_call" | custom-call | flops 1879048192 | bytes 11010048 | tf_op jit(solution)/shard_map/hidden/pallas_call | solution.py:54
  208.9 2.6 collective-permute-done.6.refs_3_
  211.5 1.7 collective-permute-done.5.refs_2_
  213.1 1.3 collective-permute-done.4.refs_1_
  215.1 5.4 %down.2 = bf16[256,1792]{1,0:T(8,128)(2,1)} custom-call(bf16[256,256]{1,0:T(8,128)(2,1)} %hidden.2.refs_0_, bf16[256,256]{1,0:T(8,128)(2,1)} %copy-done.14, bf16[256,256]{1,0:T(8,128)(2,1)} %copy-done.13, bf16[256,256]{1,0:T(8,128)(2,1)} %copy-done.11, bf16[256,1792]{1,0:T(8,128)(2,1)} %get-tuple-element.11.refs_4_, bf16[256,1792]{1,0:T(8,128)(2,1)} %copy-done.2, ...), custom_call_target="tpu_custom_call" | custom-call | flops 939524096 | bytes 5111808 | tf_op jit(solution)/shard_map/down/pallas_call | solution.py:88
  220.5 2.5 reshape.114
  223.1 14.1 %all-to-all-start.1 = ((bf16[64,4,1792]{2,1,0:T(4,128)(2,1)}), bf16[64,4,1792]{2,1,0:T(4,128)(2,1)S(1)}, u32[]{:S(2)}, u32[]{:S(2)}) async-start(bf16[64,4,1792]{2,1,0:T(4,128)(2,1)} %reshape.114), calls=%async_computation.1 | async-start | bytes 1835008 | tf_op jit(solution)/shard_map/all_to_all | solution.py:117
  238.1 24.9 %all-to-all-done.1 = bf16[64,4,1792]{2,1,0:T(4,128)(2,1)S(1)} async-done(((bf16[64,4,1792]{2,1,0:T(4,128)(2,1)}), bf16[64,4,1792]{2,1,0:T(4,128)(2,1)S(1)}, u32[]{:S(2)}, u32[]{:S(2)}) %all-to-all-start.1) | async-done | bytes 917536 | tf_op jit(solution)/shard_map/all_to_all | solution.py:117
  (84 shorter events, 17.2 us)
Async XLA Ops:
  3.9 38.7 %all-to-all-start.2 = ((bf16[64,4,1792]{2,1,0:T(4,128)(2,1)}), bf16[64,4,1792]{2,1,0:T(4,128)(2,1)S(1)}, u32[]{:S(2)}, u32[]{:S(2)}) async-start(bf16[64,4,1792]{2,1,0:T(4,128)(2,1)} %reshape.116), calls=%async_computation.2 | async-start | bytes 1835008 | tf_op jit(solution)/shard_map/all_to_all | solution.py:117
  42.6 108.2 %all-to-all-start = ((bf16[64,4,1792]{2,1,0:T(4,128)(2,1)}), bf16[64,4,1792]{2,1,0:T(4,128)(2,1)}, u32[]{:S(2)}, u32[]{:S(2)}) async-start(bf16[64,4,1792]{2,1,0:T(4,128)(2,1)} %reshape.112), calls=%async_computation | async-start | bytes 1835008 | tf_op jit(solution)/shard_map/all_to_all | solution.py:117
  50.2 22.2 %collective-permute-start.11 = (bf16[256,1792]{1,0:T(8,128)(2,1)}, bf16[256,1792]{1,0:T(8,128)(2,1)}, u32[]{:S(2)}, u32[]{:S(2)}) collective-permute-start(bf16[256,1792]{1,0:T(8,128)(2,1)} %reshape.117.mine), channel_id=1, source_target_pairs={{0,3},{1,0},{2,1},{3,2},{4,7},{5,4},{6,5},{7,6},{8,11},{9,8},{10,9... | collective-permute-start | bytes 2752520 | tf_op jit(solution)/shard_map/ppermute | solution.py:113
  52.9 24.0 %collective-permute-start.10 = (bf16[256,1792]{1,0:T(8,128)(2,1)}, bf16[256,1792]{1,0:T(8,128)(2,1)}, u32[]{:S(2)}, u32[]{:S(2)}) collective-permute-start(bf16[256,1792]{1,0:T(8,128)(2,1)} %reshape.117.mine), channel_id=1, source_target_pairs={{0,1},{1,2},{2,3},{3,0},{4,5},{5,6},{6,7},{7,4},{8,9},{9,10},{10,1... | collective-permute-start | bytes 2752520 | tf_op jit(solution)/shard_map/ppermute | solution.py:113
  52.9 25.2 %copy-start.16 = (s32[4]{0:T(128)S(1)}, s32[4]{0:T(128)}, u32[]{:S(2)}) copy-start(s32[4]{0:T(128)} %constant.100.clone) | copy-start | bytes 52
  56.8 76.4 %collective-permute-start.9 = (bf16[256,1792]{1,0:T(8,128)(2,1)}, bf16[256,1792]{1,0:T(8,128)(2,1)S(1)}, u32[]{:S(2)}, u32[]{:S(2)}) collective-permute-start(bf16[256,1792]{1,0:T(8,128)(2,1)} %get-tuple-element.9), channel_id=1, source_target_pairs={{0,3},{1,0},{2,1},{3,2},{4,7},{5,4},{6,5},{7,6},{8,11},{9,8},{10,9... | collective-permute-start | bytes 2752520 | tf_op jit(solution)/shard_map/ppermute | solution.py:113
  59.5 74.3 %collective-permute-start.7 = (bf16[256,1792]{1,0:T(8,128)(2,1)}, bf16[256,1792]{1,0:T(8,128)(2,1)S(1)}, u32[]{:S(2)}, u32[]{:S(2)}) collective-permute-start(bf16[256,1792]{1,0:T(8,128)(2,1)} %get-tuple-element.10), channel_id=1, source_target_pairs={{0,1},{1,2},{2,3},{3,0},{4,5},{5,6},{6,7},{7,4},{8,9},{9,10},{10,1... | collective-permute-start | bytes 2752520 | tf_op jit(solution)/shard_map/ppermute | solution.py:113
  59.5 74.3 %collective-permute-start.8 = (bf16[256,1792]{1,0:T(8,128)(2,1)}, bf16[256,1792]{1,0:T(8,128)(2,1)S(1)}, u32[]{:S(2)}, u32[]{:S(2)}) collective-permute-start(bf16[256,1792]{1,0:T(8,128)(2,1)} %get-tuple-element.12), channel_id=1, source_target_pairs={{0,2},{1,3},{2,0},{3,1},{4,6},{5,7},{6,4},{7,5},{8,10},{9,11},{10,... | collective-permute-start | bytes 2752520 | tf_op jit(solution)/shard_map/ppermute | solution.py:113
  73.4 48.0 %collective-permute-start.13 = (bf16[128,1792]{1,0:T(8,128)(2,1)S(1)}, bf16[128,1792]{1,0:T(8,128)(2,1)S(1)}, u32[]{:S(2)}, u32[]{:S(2)}) collective-permute-start(bf16[128,1792]{1,0:T(8,128)(2,1)S(1)} %slice.46), channel_id=1, source_target_pairs={{0,3},{1,0},{2,1},{3,2},{4,7},{5,4},{6,5},{7,6},{8,11},{9,8},{10,9... | collective-permute-start | bytes 1376264 | tf_op jit(solution)/shard_map/ppermute | solution.py:113
  78.0 46.7 %collective-permute-start.12 = (bf16[128,1792]{1,0:T(8,128)(2,1)S(1)}, bf16[128,1792]{1,0:T(8,128)(2,1)}, u32[]{:S(2)}, u32[]{:S(2)}) collective-permute-start(bf16[128,1792]{1,0:T(8,128)(2,1)S(1)} %slice.45), channel_id=1, source_target_pairs={{0,1},{1,2},{2,3},{3,0},{4,5},{5,6},{6,7},{7,4},{8,9},{9,10},{10,1... | collective-permute-start | bytes 1376264 | tf_op jit(solution)/shard_map/ppermute | solution.py:113
  121.4 3.2 %copy-start.7 = (bf16[128,1792]{1,0:T(8,128)(2,1)}, bf16[128,1792]{1,0:T(8,128)(2,1)S(1)}, u32[]{:S(2)}) copy-start(bf16[128,1792]{1,0:T(8,128)(2,1)S(1)} %collective-permute-done.13.rear) | copy-start | bytes 1376260
  132.2 4.0 %collective-permute-start.16 = (bf16[256,256]{1,0:T(8,128)(2,1)}, bf16[256,256]{1,0:T(8,128)(2,1)S(1)}, u32[]{:S(2)}, u32[]{:S(2)}) collective-permute-start(bf16[256,256]{1,0:T(8,128)(2,1)} %hidden.3.refs_0_), channel_id=1, source_target_pairs={{0,3},{1,0},{2,1},{3,2},{4,7},{5,4},{6,5},{7,6},{8,11},{9,8},{10,9... | collective-permute-start | bytes 393224 | tf_op jit(solution)/shard_map/ppermute | solution.py:113
  133.2 5.6 %collective-permute-start.15 = (bf16[256,256]{1,0:T(8,128)(2,1)}, bf16[256,256]{1,0:T(8,128)(2,1)S(1)}, u32[]{:S(2)}, u32[]{:S(2)}) collective-permute-start(bf16[256,256]{1,0:T(8,128)(2,1)} %hidden.3.refs_0_), channel_id=1, source_target_pairs={{0,2},{1,3},{2,0},{3,1},{4,6},{5,7},{6,4},{7,5},{8,10},{9,11},{10,... | collective-permute-start | bytes 393224 | tf_op jit(solution)/shard_map/ppermute | solution.py:113
  133.2 9.1 %copy-start.1 = (bf16[256,1792]{1,0:T(8,128)(2,1)}, bf16[256,1792]{1,0:T(8,128)(2,1)S(1)}, u32[]{:S(2)}) copy-start(bf16[256,1792]{1,0:T(8,128)(2,1)S(1)} %collective-permute-done.9.refs_7_) | copy-start | bytes 2752516
  133.2 9.1 %collective-permute-start.14 = (bf16[256,256]{1,0:T(8,128)(2,1)}, bf16[256,256]{1,0:T(8,128)(2,1)S(1)}, u32[]{:S(2)}, u32[]{:S(2)}) collective-permute-start(bf16[256,256]{1,0:T(8,128)(2,1)} %hidden.3.refs_0_), channel_id=1, source_target_pairs={{0,1},{1,2},{2,3},{3,0},{4,5},{5,6},{6,7},{7,4},{8,9},{9,10},{10,1... | collective-permute-start | bytes 393224 | tf_op jit(solution)/shard_map/ppermute | solution.py:113
  133.8 8.5 %copy-start.2 = (bf16[256,1792]{1,0:T(8,128)(2,1)}, bf16[256,1792]{1,0:T(8,128)(2,1)S(1)}, u32[]{:S(2)}) copy-start(bf16[256,1792]{1,0:T(8,128)(2,1)S(1)} %collective-permute-done.7.refs_5_) | copy-start | bytes 2752516
  133.8 8.5 %copy-start.3 = (bf16[256,1792]{1,0:T(8,128)(2,1)}, bf16[256,1792]{1,0:T(8,128)(2,1)S(1)}, u32[]{:S(2)}) copy-start(bf16[256,1792]{1,0:T(8,128)(2,1)S(1)} %collective-permute-done.8.refs_6_) | copy-start | bytes 2752516
  136.2 6.1 %copy-start.9 = (bf16[256,256]{1,0:T(8,128)(2,1)}, bf16[256,256]{1,0:T(8,128)(2,1)S(1)}, u32[]{:S(2)}) copy-start(bf16[256,256]{1,0:T(8,128)(2,1)S(1)} %collective-permute-done.16.refs_3_) | copy-start | bytes 393220
  138.8 3.5 %copy-start.10 = (bf16[256,256]{1,0:T(8,128)(2,1)}, bf16[256,256]{1,0:T(8,128)(2,1)S(1)}, u32[]{:S(2)}) copy-start(bf16[256,256]{1,0:T(8,128)(2,1)S(1)} %collective-permute-done.15.refs_2_) | copy-start | bytes 393220
  150.8 72.2 %all-to-all-start.3 = ((bf16[64,4,1792]{2,1,0:T(4,128)(2,1)}), bf16[64,4,1792]{2,1,0:T(4,128)(2,1)S(1)}, u32[]{:S(2)}, u32[]{:S(2)}) async-start(bf16[64,4,1792]{2,1,0:T(4,128)(2,1)} %reshape.118), calls=%async_computation.3 | async-start | bytes 1835008 | tf_op jit(solution)/shard_map/all_to_all | solution.py:117
  163.8 36.1 %copy-start.4 = (bf16[256,1792]{1,0:T(8,128)(2,1)}, bf16[256,1792]{1,0:T(8,128)(2,1)S(1)}, u32[]{:S(2)}) copy-start(bf16[256,1792]{1,0:T(8,128)(2,1)S(1)} %reshape.113.mine) | copy-start | bytes 2752516
  163.8 21.5 %collective-permute-start.1 = (bf16[256,1792]{1,0:T(8,128)(2,1)S(1)}, bf16[256,1792]{1,0:T(8,128)(2,1)S(1)}, u32[]{:S(2)}, u32[]{:S(2)}) collective-permute-start(bf16[256,1792]{1,0:T(8,128)(2,1)S(1)} %reshape.113.mine), channel_id=1, source_target_pairs={{0,3},{1,0},{2,1},{3,2},{4,7},{5,4},{6,5},{7,6},{8,11},{9,8},{10,9... | collective-permute-start | bytes 2752520 | tf_op jit(solution)/shard_map/ppermute | solution.py:113
  164.3 22.8 %collective-permute-start = (bf16[256,1792]{1,0:T(8,128)(2,1)S(1)}, bf16[256,1792]{1,0:T(8,128)(2,1)S(1)}, u32[]{:S(2)}, u32[]{:S(2)}) collective-permute-start(bf16[256,1792]{1,0:T(8,128)(2,1)S(1)} %reshape.113.mine), channel_id=1, source_target_pairs={{0,1},{1,2},{2,3},{3,0},{4,5},{5,6},{6,7},{7,4},{8,9},{9,10},{10,1... | collective-permute-start | bytes 2752520 | tf_op jit(solution)/shard_map/ppermute | solution.py:113
  185.4 14.6 %copy-start.5 = (bf16[256,1792]{1,0:T(8,128)(2,1)}, bf16[256,1792]{1,0:T(8,128)(2,1)S(1)}, u32[]{:S(2)}) copy-start(bf16[256,1792]{1,0:T(8,128)(2,1)S(1)} %collective-permute-done.1.right) | copy-start | bytes 2752516
  185.4 11.0 %collective-permute-start.3 = (bf16[128,1792]{1,0:T(8,128)(2,1)S(1)}, bf16[128,1792]{1,0:T(8,128)(2,1)S(1)}, u32[]{:S(2)}, u32[]{:S(2)}) collective-permute-start(bf16[128,1792]{1,0:T(8,128)(2,1)S(1)} %slice.42), channel_id=1, source_target_pairs={{0,3},{1,0},{2,1},{3,2},{4,7},{5,4},{6,5},{7,6},{8,11},{9,8},{10,9... | collective-permute-start | bytes 1376264 | tf_op jit(solution)/shard_map/ppermute | solution.py:113
  188.0 11.9 %collective-permute-start.2 = (bf16[128,1792]{1,0:T(8,128)(2,1)S(1)}, bf16[128,1792]{1,0:T(8,128)(2,1)}, u32[]{:S(2)}, u32[]{:S(2)}) collective-permute-start(bf16[128,1792]{1,0:T(8,128)(2,1)S(1)} %slice.41), channel_id=1, source_target_pairs={{0,1},{1,2},{2,3},{3,0},{4,5},{5,6},{6,7},{7,4},{8,9},{9,10},{10,1... | collective-permute-start | bytes 1376264 | tf_op jit(solution)/shard_map/ppermute | solution.py:113
  196.3 3.6 %copy-start.8 = (bf16[128,1792]{1,0:T(8,128)(2,1)}, bf16[128,1792]{1,0:T(8,128)(2,1)S(1)}, u32[]{:S(2)}) copy-start(bf16[128,1792]{1,0:T(8,128)(2,1)S(1)} %collective-permute-done.3.rear) | copy-start | bytes 1376260
  207.5 29.8 %copy-start.15 = (f32[32,8]{0,1:T(8,128)S(1)}, f32[32,8]{0,1:T(8,128)}, u32[]{:S(2)}) copy-start(f32[32,8]{0,1:T(8,128)} %param.9) | copy-start | bytes 3076
  207.5 4.0 %collective-permute-start.6 = (bf16[256,256]{1,0:T(8,128)(2,1)}, bf16[256,256]{1,0:T(8,128)(2,1)S(1)}, u32[]{:S(2)}, u32[]{:S(2)}) collective-permute-start(bf16[256,256]{1,0:T(8,128)(2,1)} %hidden.2.refs_0_), channel_id=1, source_target_pairs={{0,3},{1,0},{2,1},{3,2},{4,7},{5,4},{6,5},{7,6},{8,11},{9,8},{10,9... | collective-permute-start | bytes 393224 | tf_op jit(solution)/shard_map/ppermute | solution.py:113
  207.5 5.7 %collective-permute-start.5 = (bf16[256,256]{1,0:T(8,128)(2,1)}, bf16[256,256]{1,0:T(8,128)(2,1)S(1)}, u32[]{:S(2)}, u32[]{:S(2)}) collective-permute-start(bf16[256,256]{1,0:T(8,128)(2,1)} %hidden.2.refs_0_), channel_id=1, source_target_pairs={{0,2},{1,3},{2,0},{3,1},{4,6},{5,7},{6,4},{7,5},{8,10},{9,11},{10,... | collective-permute-start | bytes 393224 | tf_op jit(solution)/shard_map/ppermute | solution.py:113
  208.2 6.3 %collective-permute-start.4 = (bf16[256,256]{1,0:T(8,128)(2,1)}, bf16[256,256]{1,0:T(8,128)(2,1)S(1)}, u32[]{:S(2)}, u32[]{:S(2)}) collective-permute-start(bf16[256,256]{1,0:T(8,128)(2,1)} %hidden.2.refs_0_), channel_id=1, source_target_pairs={{0,1},{1,2},{2,3},{3,0},{4,5},{5,6},{6,7},{7,4},{8,9},{9,10},{10,1... | collective-permute-start | bytes 393224 | tf_op jit(solution)/shard_map/ppermute | solution.py:113
  223.1 39.9 %all-to-all-start.1 = ((bf16[64,4,1792]{2,1,0:T(4,128)(2,1)}), bf16[64,4,1792]{2,1,0:T(4,128)(2,1)S(1)}, u32[]{:S(2)}, u32[]{:S(2)}) async-start(bf16[64,4,1792]{2,1,0:T(4,128)(2,1)} %reshape.114), calls=%async_computation.1 | async-start | bytes 1835008 | tf_op jit(solution)/shard_map/all_to_all | solution.py:117
  (6 other events, 8.9 us)

commit v3 on v2

v3 whole, which is shorter than its diff:
```python
import functools

import jax
import jax.numpy as jnp
from jax import lax
from jax.experimental import pallas as pl
from jax.experimental.pallas import tpu as pltpu
from jax.sharding import PartitionSpec as P


SIZES = (4, 4)
F32 = jnp.float32
BF16 = jnp.bfloat16


def vmem():
    return pl.BlockSpec(memory_space=pltpu.VMEM)


def begin_kernel(order_ref, *refs):
    blocks, (gate_ref, up_ref, gate_acc, up_acc) = refs[:3], refs[3:]
    step = pl.program_id(0)

    @pl.when(step == 0)
    def _():
        gate_acc[...] = jnp.zeros_like(gate_acc)
        up_acc[...] = jnp.zeros_like(up_acc)

    for i, block in enumerate(blocks):

        @pl.when(step == i)
        def _(block=block):
            gate_acc[...] += jnp.dot(block[...], gate_ref[...], preferred_element_type=F32)
            up_acc[...] += jnp.dot(block[...], up_ref[...], preferred_element_type=F32)


def finish_kernel(order_ref, front, rear, gate_ref, up_ref, gate_acc, up_acc, out_ref):
    rows = front.shape[0]
    for i, block in enumerate((front, rear)):
        at = pl.ds(i * rows, rows)
        gate = gate_acc[at, :] + jnp.dot(block[...], gate_ref[...], preferred_element_type=F32)
        up = up_acc[at, :] + jnp.dot(block[...], up_ref[...], preferred_element_type=F32)
        out_ref[at, :] = (gate / (1.0 + jnp.exp(-gate)) * up).astype(BF16)


def hidden_of(order, blocks, gate_proj, up_proj):
    rows, depth = blocks[0].shape
    cols = gate_proj.shape[2]
    acc = pl.BlockSpec((rows, cols), lambda k, order: (0, 0))

    def call(kernel, first, count, given, more, outs):
        weight = pl.BlockSpec((None, depth, cols), lambda k, order: (0, order[first + k], 0))
        return pl.pallas_call(
            kernel,
            grid_spec=pltpu.PrefetchScalarGridSpec(
                num_scalar_prefetch=1,
                grid=(count,),
                in_specs=[pl.BlockSpec(b.shape, lambda k, order: (0, 0)) for b in given]
                + [weight, weight]
                + [acc] * len(more),
                out_specs=[acc] * len(outs),
            ),
            out_shape=[jax.ShapeDtypeStruct((rows, cols), t) for t in outs],
            cost_estimate=pl.CostEstimate(
                flops=4 * count * rows * depth * cols,
                bytes_accessed=2 * count * depth * (rows + 2 * cols),
                transcendentals=rows * cols,
            ),
        )(order, *given, gate_proj, up_proj, *more)

    partial = call(begin_kernel, 0, 3, blocks[:3], [], [F32, F32])
    return call(finish_kernel, 3, 1, blocks[3:], partial, [BF16])[0]


def down_kernel(pairs, *refs):
    out = refs[-1]
    experts, share, width = out.shape
    tile = width // 2

    @pl.loop(0, 2)
    def _(k):
        at = pl.ds(pl.multiple_of(k * tile, tile), tile)
        total = jnp.dot(refs[0][...], refs[pairs][:, at], preferred_element_type=F32)
        for i in range(1, pairs):
            total += jnp.dot(refs[i][...], refs[pairs + i][:, at], preferred_element_type=F32)
        out[:, :, at] = total.reshape(experts, share, tile).astype(BF16)


def down_of(hiddens, downs, experts):
    rows, inner = hiddens[0].shape
    width = downs[0].shape[1]
    n = len(hiddens)
    return pl.pallas_call(
        functools.partial(down_kernel, n),
        in_specs=[vmem()] * (2 * n),
        out_specs=vmem(),
        out_shape=jax.ShapeDtypeStruct((experts, rows // experts, width), BF16),
        cost_estimate=pl.CostEstimate(
            flops=2 * n * rows * inner * width,
            bytes_accessed=2 * n * inner * (rows + width) + 2 * rows * width,
            transcendentals=0,
        ),
        name="down",
    )(*hiddens, *downs)


def layer(tokens, routes, route_weights, gate_proj, up_proj, down_proj):
    w_down = down_proj[0]
    tok_count, width = tokens.shape
    fanout = routes.shape[1]
    experts = lax.axis_size("ep")
    parts = lax.axis_size("tp")
    tp = lax.axis_index("tp")
    capacity = sum(SIZES)
    order = (tp + jnp.array([0, parts - 1, 1, 2], jnp.int32)) % parts

    def over_y(value, by):
        return lax.ppermute(value, "tp", [(i, (i + by) % parts) for i in range(parts)])

    def exchange(blocks):
        return lax.all_to_all(blocks, "ep", split_axis=0, concat_axis=0, tiled=True)

    downs = []
    for by in range(parts):
        start = (tp + by) % parts * width
        piece = lax.dynamic_slice_in_dim(w_down, start, width, axis=1)
        downs.append(piece if by == 0 else over_y(piece, by))

    flat_ids = routes.reshape(-1)
    onehot = (flat_ids[:, None] == jnp.arange(experts, dtype=jnp.int32)[None, :]).astype(jnp.int32)
    before = jnp.cumsum(onehot, axis=0) - onehot
    position = jnp.sum(before * onehot, axis=1)
    target = (flat_ids * capacity + position).reshape(tok_count, fanout)

    mixed = jnp.zeros((tok_count, width), F32)
    first = 0
    for size in SIZES:
        row = jnp.arange(experts * size, dtype=jnp.int32)
        slot = row // size * capacity + first + row % size
        first += size
        select = jnp.any(target[None, :, :] == slot[:, None, None], axis=2).astype(BF16)
        sending = jnp.dot(select, tokens, preferred_element_type=F32).astype(BF16)
        landed = exchange(sending.reshape(experts, size, width))
        mine = landed.reshape(-1, width)
        cut = mine.shape[0] // 2
        left = over_y(mine, 1)
        right = over_y(mine, -1)
        left_cut, right_cut = left[:cut], right[cut:]
        front = over_y(left_cut, 1)
        rear = over_y(right_cut, -1)
        hidden = hidden_of(order, [mine, left, right, front, rear], gate_proj, up_proj)
        hiddens = [hidden] + [over_y(hidden, by) for by in range(1, parts)]
        out = down_of(hiddens, downs, experts)
        back = exchange(out).reshape(-1, width)
        weight = jnp.sum(
            jnp.where(target[:, :, None] == slot[None, None, :], route_weights[:, :, None], 0.0), axis=1
        )
        high = lax.reduce_precision(weight, 8, 7)
        both = jnp.concatenate([high, weight - high]).astype(BF16)
        both = jnp.dot(both, back, preferred_element_type=F32)
        mixed = mixed + (both[:tok_count] + both[tok_count:])
    return mixed.astype(BF16)


def solution(mesh):
    in_specs = (
        P("ep", "tp"),
        P("ep", None),
        P("ep", None),
        P("ep", None, "tp"),
        P("ep", None, "tp"),
        P("ep", "tp", None),
    )
    out_specs = P("ep", "tp")
    return jax.shard_map(layer, mesh=mesh, in_specs=in_specs, out_specs=out_specs, check_vma=False)
```

time: 265 us -> 251 us (0.947)
  waiting for transfers between devices: 153 us -> 138 us
  local copies, waits for them, and re-layouts: 20.2 us -> 15.8 us
  Pallas kernels: 25.8 us -> 30.1 us
    ppermute x17, waiting for transfers between devices: 104 us -> 89 us  [over_y(): lax.ppermute(value, 'tp', [(i, (i + by) % parts) for i in range(parts)])]
    reshape x8 -> x6, local copies, waits for them, and re-layouts: 10.6 us -> 4.58 us  [the longest x2 2.3 us: layer(): landed = exchange(sending.reshape(experts, size, width))]
    pallas_call x2 -> x4, Pallas kernels: 15 us -> 20.8 us  [call(): pl.pallas_call(kernel, grid_spec=pltpu.PrefetchScalarGridSpec(num_scalar_...]
  transfers between devices with their start and end apart: 21 -> 21, of which waited for: 14 -> 14; matrix products, arithmetic and copies ran while one was open for 6% -> 5% of each run, Pallas kernels for 10% -> 12%
where the time goes in v3:
time: 251 us; the launch traced here: 250 us
  waiting for transfers between devices  138 us (55%)
  starting transfers between devices  62.4 us (25%)
  Pallas kernels  30.1 us (12%)
  local copies, waits for them, and re-layouts  15.8 us (6%)
    ppermute x17, waiting for transfers between devices, over_y(): lax.ppermute(value, 'tp', [(i, (i + by) % parts) for i in range(parts)])  89 us
    all_to_all x4, waiting for transfers between devices, exchange(): return lax.all_to_all(blocks, 'ep', split_axis=0, concat_axis=0, tiled=True)  49 us
    all_to_all x4, starting transfers between devices, exchange(): return lax.all_to_all(blocks, 'ep', split_axis=0, concat_axis=0, tiled=True)  45.6 us
    pallas_call x4, Pallas kernels, call(): pl.pallas_call(kernel, grid_spec=pltpu.PrefetchScalarGridSpec(num_scalar_...  20.8 us
    ppermute x17, starting transfers between devices, over_y(): lax.ppermute(value, 'tp', [(i, (i + by) % parts) for i in range(parts)])  16.9 us
    pallas_call x2, Pallas kernels, down_of(): pl.pallas_call(functools.partial(down_kernel, n), in_specs=[vmem()] * (2...  9.27 us
  transfers between devices with their start and end apart: 21, of which 14 were waited for; matrix products, arithmetic and copies ran while one was open for 5% of the time, Pallas kernels for 12%

profile of v3, /device:TPU:1, one launch (start us, length us, event | category | flops | bytes accessed | tf_op | source)
XLA Modules:
  0.0 250.4 jit_solution(15058356479649495532)
XLA Ops:
  2.8 1.2 reshape.106
  3.9 13.0 %all-to-all-start = ((bf16[64,4,1792]{2,1,0:T(4,128)(2,1)}), bf16[64,4,1792]{2,1,0:T(4,128)(2,1)S(1)}, u32[]{:S(2)}, u32[]{:S(2)}) async-start(bf16[64,4,1792]{2,1,0:T(4,128)(2,1)} %reshape.106), calls=%async_computation | async-start | bytes 1835008 | tf_op jit(solution)/shard_map/all_to_all | solution.py:121
  17.3 1.1 reshape.109
  18.5 24.1 %all-to-all-done = bf16[64,4,1792]{2,1,0:T(4,128)(2,1)S(1)} async-done(((bf16[64,4,1792]{2,1,0:T(4,128)(2,1)}), bf16[64,4,1792]{2,1,0:T(4,128)(2,1)S(1)}, u32[]{:S(2)}, u32[]{:S(2)}) %all-to-all-start) | async-done | bytes 917536 | tf_op jit(solution)/shard_map/all_to_all | solution.py:121
  42.6 6.4 %all-to-all-start.2 = ((bf16[64,4,1792]{2,1,0:T(4,128)(2,1)}), bf16[64,4,1792]{2,1,0:T(4,128)(2,1)}, u32[]{:S(2)}, u32[]{:S(2)}) async-start(bf16[64,4,1792]{2,1,0:T(4,128)(2,1)} %reshape.109), calls=%async_computation.2 | async-start | bytes 1835008 | tf_op jit(solution)/shard_map/all_to_all | solution.py:121
  49.2 2.8 %collective-permute-start.2 = (bf16[256,1792]{1,0:T(8,128)(2,1)S(1)}, bf16[256,1792]{1,0:T(8,128)(2,1)}, u32[]{:S(2)}, u32[]{:S(2)}) collective-permute-start(bf16[256,1792]{1,0:T(8,128)(2,1)S(1)} %reshape.107.refs_0_), channel_id=1, source_target_pairs={{0,3},{1,0},{2,1},{3,2},{4,7},{5,4},{6,5},{7,6},{8,11},{9,8},{10,9... | collective-permute-start | bytes 2752520 | tf_op jit(solution)/shard_map/ppermute | solution.py:118
  52.1 3.9 %dynamic-slice_bitcast_fusion = (bf16[256,1792]{1,0:T(8,128)(2,1)}, bf16[256,1792]{1,0:T(8,128)(2,1)}, bf16[256,1792]{1,0:T(8,128)(2,1)}, bf16[256,1792]{1,0:T(8,128)(2,1)}) fusion(bf16[1,256,7168]{2,1,0:T(8,128)(2,1)} %param.12, s32[]{:T(128)S(6)} %select_n.109, s32[]{:T(128)S(6)} %select_n.105, s32[]{:T(128)S(6)} %select_n.103, s32[]{:T(128)S(6)} %select_n.107), kind=kLoop, calls=%fused_computation.2 | loop fusion | bytes 7340048 | tf_op jit(solution)/shard_map/dynamic_slice | solution.py:126
  56.0 2.7 %collective-permute-start.9 = (bf16[256,1792]{1,0:T(8,128)(2,1)}, bf16[256,1792]{1,0:T(8,128)(2,1)S(1)}, u32[]{:S(2)}, u32[]{:S(2)}) collective-permute-start(bf16[256,1792]{1,0:T(8,128)(2,1)} %get-tuple-element.17), channel_id=1, source_target_pairs={{0,3},{1,0},{2,1},{3,2},{4,7},{5,4},{6,5},{7,6},{8,11},{9,8},{10,9... | collective-permute-start | bytes 2752520 | tf_op jit(solution)/shard_map/ppermute | solution.py:118
  58.6 1.3 collective-permute-start.8
  59.9 11.3 %collective-permute-done.2.refs_2_ = bf16[256,1792]{1,0:T(8,128)(2,1)} collective-permute-done((bf16[256,1792]{1,0:T(8,128)(2,1)S(1)}, bf16[256,1792]{1,0:T(8,128)(2,1)}, u32[]{:S(2)}, u32[]{:S(2)}) %collective-permute-start.2) | collective-permute-done | bytes 917536 | tf_op jit(solution)/shard_map/ppermute | solution.py:118
  72.3 3.6 %collective-permute-start.3 = (bf16[128,1792]{1,0:T(8,128)(2,1)S(1)}, bf16[128,1792]{1,0:T(8,128)(2,1)}, u32[]{:S(2)}, u32[]{:S(2)}) collective-permute-start(bf16[128,1792]{1,0:T(8,128)(2,1)S(1)} %slice.42), channel_id=1, source_target_pairs={{0,3},{1,0},{2,1},{3,2},{4,7},{5,4},{6,5},{7,6},{8,11},{9,8},{10,9... | collective-permute-start | bytes 1376264 | tf_op jit(solution)/shard_map/ppermute | solution.py:118
  77.6 6.5 %shard_map.73 = (f32[256,256]{1,0:T(8,128)}, f32[256,256]{1,0:T(8,128)}) custom-call(s32[4]{0:T(128)} %and_select_fusion.order_ref, bf16[256,1792]{1,0:T(8,128)(2,1)} %copy-done.1, bf16[256,1792]{1,0:T(8,128)(2,1)} %collective-permute-done.refs_1_, bf16[256,1792]{1,0:T(8,128)(2,1)} %collective-permute-done.2.refs_2_, bf16[1,7168,256]{2,1,0:T(8,128)(2,1)} %gate_ref.3, ...), custom_call_target="tpu_custom_call" | custom-call | flops 1409286144 | bytes 8257536 | tf_op jit(solution)/shard_map/pallas_call | solution.py:53
  84.1 36.3 %collective-permute-done.3.rear = bf16[128,1792]{1,0:T(8,128)(2,1)} collective-permute-done((bf16[128,1792]{1,0:T(8,128)(2,1)S(1)}, bf16[128,1792]{1,0:T(8,128)(2,1)}, u32[]{:S(2)}, u32[]{:S(2)}) %collective-permute-start.3) | collective-permute-done | bytes 458784 | tf_op jit(solution)/shard_map/ppermute | solution.py:118
  120.4 3.1 %collective-permute-done.1.front = bf16[128,1792]{1,0:T(8,128)(2,1)S(1)} collective-permute-done((bf16[128,1792]{1,0:T(8,128)(2,1)S(1)}, bf16[128,1792]{1,0:T(8,128)(2,1)S(1)}, u32[]{:S(2)}, u32[]{:S(2)}) %collective-permute-start.1) | collective-permute-done | bytes 458784 | tf_op jit(solution)/shard_map/ppermute | solution.py:118
  124.3 3.8 %shard_map.74.refs_0_ = bf16[256,256]{1,0:T(8,128)(2,1)} custom-call(s32[4]{0:T(128)} %and_select_fusion.order_ref, bf16[128,1792]{1,0:T(8,128)(2,1)} %copy-done.7, bf16[128,1792]{1,0:T(8,128)(2,1)} %collective-permute-done.3.rear, bf16[1,7168,256]{2,1,0:T(8,128)(2,1)} %gate_ref.3, bf16[1,7168,256]{2,1,0:T(8,128)(2,1)} %up_ref.3, ...), custom_call_target="tpu_custom_call" | custom-call | flops 469762048 | bytes 2752512 | tf_op jit(solution)/shard_map/pallas_call | solution.py:53
  129.7 2.5 collective-permute-done.6.refs_3_
  132.2 2.0 collective-permute-done.5.refs_2_
  134.2 2.8 %collective-permute-done.4.refs_1_ = bf16[256,256]{1,0:T(8,128)(2,1)S(1)} collective-permute-done((bf16[256,256]{1,0:T(8,128)(2,1)}, bf16[256,256]{1,0:T(8,128)(2,1)S(1)}, u32[]{:S(2)}, u32[]{:S(2)}) %collective-permute-start.4) | collective-permute-done | bytes 131104 | tf_op jit(solution)/shard_map/ppermute | solution.py:118
  137.7 4.6 %down.2 = bf16[64,4,1792]{2,1,0:T(4,128)(2,1)} custom-call(bf16[256,256]{1,0:T(8,128)(2,1)} %shard_map.74.refs_0_, bf16[256,256]{1,0:T(8,128)(2,1)} %copy-done.11, bf16[256,256]{1,0:T(8,128)(2,1)} %copy-done.9, bf16[256,256]{1,0:T(8,128)(2,1)} %copy-done.8, bf16[256,1792]{1,0:T(8,128)(2,1)} %get-tuple-element.19.refs_4_, bf16[256,1792]{1,0:T(8,128)(2,1)} %copy-done.4, ...), custom_call_target="tpu_custom_call" | custom-call | flops 939524096 | bytes 5111808 | tf_op jit(solution)/shard_map/down/pallas_call | solution.py:93
  142.3 12.0 %all-to-all-start.1 = ((bf16[64,4,1792]{2,1,0:T(4,128)(2,1)}), bf16[64,4,1792]{2,1,0:T(4,128)(2,1)S(1)}, u32[]{:S(2)}, u32[]{:S(2)}) async-start(bf16[64,4,1792]{2,1,0:T(4,128)(2,1)} %down.2), calls=%async_computation.1 | async-start | bytes 1835008 | tf_op jit(solution)/shard_map/all_to_all | solution.py:121
  154.3 1.7 reshape.110.refs_0_
  157.6 20.0 %collective-permute-done.12.refs_2_ = bf16[256,1792]{1,0:T(8,128)(2,1)S(1)} collective-permute-done((bf16[256,1792]{1,0:T(8,128)(2,1)S(1)}, bf16[256,1792]{1,0:T(8,128)(2,1)S(1)}, u32[]{:S(2)}, u32[]{:S(2)}) %collective-permute-start.12) | collective-permute-done | bytes 917536 | tf_op jit(solution)/shard_map/ppermute | solution.py:118
  177.6 1.9 collective-permute-start.13
  181.2 6.6 %shard_map.75 = (f32[256,256]{1,0:T(8,128)}, f32[256,256]{1,0:T(8,128)}) custom-call(s32[4]{0:T(128)} %and_select_fusion.order_ref, bf16[256,1792]{1,0:T(8,128)(2,1)} %copy-done.2, bf16[256,1792]{1,0:T(8,128)(2,1)} %copy-done.6, bf16[256,1792]{1,0:T(8,128)(2,1)} %copy-done.5, bf16[1,7168,256]{2,1,0:T(8,128)(2,1)} %gate_ref.3, bf16[1,7168,256]{2,1,0:T(8,128)(2,1)} %up_ref.3), custom_call_target="tpu_custom_call" | custom-call | flops 1409286144 | bytes 8257536 | tf_op jit(solution)/shard_map/pallas_call | solution.py:53
  188.5 4.7 %collective-permute-done.11.front = bf16[128,1792]{1,0:T(8,128)(2,1)} collective-permute-done((bf16[128,1792]{1,0:T(8,128)(2,1)}, bf16[128,1792]{1,0:T(8,128)(2,1)}, u32[]{:S(2)}, u32[]{:S(2)}) %collective-permute-start.11) | collective-permute-done | bytes 458784 | tf_op jit(solution)/shard_map/ppermute | solution.py:118
  193.2 3.8 %shard_map.76.refs_0_ = bf16[256,256]{1,0:T(8,128)(2,1)} custom-call(s32[4]{0:T(128)} %and_select_fusion.order_ref, bf16[128,1792]{1,0:T(8,128)(2,1)} %collective-permute-done.11.front, bf16[128,1792]{1,0:T(8,128)(2,1)} %collective-permute-done.13.rear, bf16[1,7168,256]{2,1,0:T(8,128)(2,1)} %gate_ref.3, bf16[1,7168,256]{2,1,0:T(8,128)(2,1)} %up_ref.3, ...), custom_call_target="tpu_custom_call" | custom-call | flops 469762048 | bytes 2752512 | tf_op jit(solution)/shard_map/pallas_call | solution.py:53
  198.5 2.6 %collective-permute-done.16.refs_3_ = bf16[256,256]{1,0:T(8,128)(2,1)S(1)} collective-permute-done((bf16[256,256]{1,0:T(8,128)(2,1)}, bf16[256,256]{1,0:T(8,128)(2,1)S(1)}, u32[]{:S(2)}, u32[]{:S(2)}) %collective-permute-start.16) | collective-permute-done | bytes 131104 | tf_op jit(solution)/shard_map/ppermute | solution.py:118
  201.1 1.6 collective-permute-done.15.refs_2_
  202.7 1.4 collective-permute-done.14.refs_1_
  204.7 4.6 %down.3 = bf16[64,4,1792]{2,1,0:T(4,128)(2,1)} custom-call(bf16[256,256]{1,0:T(8,128)(2,1)} %shard_map.76.refs_0_, bf16[256,256]{1,0:T(8,128)(2,1)} %copy-done.13, bf16[256,256]{1,0:T(8,128)(2,1)} %copy-done.12, bf16[256,256]{1,0:T(8,128)(2,1)} %copy-done.10, bf16[256,1792]{1,0:T(8,128)(2,1)} %get-tuple-element.19.refs_4_, bf16[256,1792]{1,0:T(8,128)(2,1)} %copy-done.4, ...), custom_call_target="tpu_custom_call" | custom-call | flops 939524096 | bytes 5111808 | tf_op jit(solution)/shard_map/down/pallas_call | solution.py:93
  209.3 14.2 %all-to-all-start.3 = ((bf16[64,4,1792]{2,1,0:T(4,128)(2,1)}), bf16[64,4,1792]{2,1,0:T(4,128)(2,1)S(1)}, u32[]{:S(2)}, u32[]{:S(2)}) async-start(bf16[64,4,1792]{2,1,0:T(4,128)(2,1)} %down.3), calls=%async_computation.3 | async-start | bytes 1835008 | tf_op jit(solution)/shard_map/all_to_all | solution.py:121
  224.4 24.9 %all-to-all-done.3 = bf16[64,4,1792]{2,1,0:T(4,128)(2,1)S(1)} async-done(((bf16[64,4,1792]{2,1,0:T(4,128)(2,1)}), bf16[64,4,1792]{2,1,0:T(4,128)(2,1)S(1)}, u32[]{:S(2)}, u32[]{:S(2)}) %all-to-all-start.3) | async-done | bytes 917536 | tf_op jit(solution)/shard_map/all_to_all | solution.py:121
  (82 shorter events, 17.3 us)
Async XLA Ops:
  0.0 2.3 copy-start
  3.9 38.7 %all-to-all-start = ((bf16[64,4,1792]{2,1,0:T(4,128)(2,1)}), bf16[64,4,1792]{2,1,0:T(4,128)(2,1)S(1)}, u32[]{:S(2)}, u32[]{:S(2)}) async-start(bf16[64,4,1792]{2,1,0:T(4,128)(2,1)} %reshape.106), calls=%async_computation | async-start | bytes 1835008 | tf_op jit(solution)/shard_map/all_to_all | solution.py:121
  42.6 99.7 %all-to-all-start.2 = ((bf16[64,4,1792]{2,1,0:T(4,128)(2,1)}), bf16[64,4,1792]{2,1,0:T(4,128)(2,1)}, u32[]{:S(2)}, u32[]{:S(2)}) async-start(bf16[64,4,1792]{2,1,0:T(4,128)(2,1)} %reshape.109), calls=%async_computation.2 | async-start | bytes 1835008 | tf_op jit(solution)/shard_map/all_to_all | solution.py:121
  49.2 6.7 %copy-start.1 = (bf16[256,1792]{1,0:T(8,128)(2,1)}, bf16[256,1792]{1,0:T(8,128)(2,1)S(1)}, u32[]{:S(2)}) copy-start(bf16[256,1792]{1,0:T(8,128)(2,1)S(1)} %reshape.107.refs_0_) | copy-start | bytes 2752516
  49.2 22.0 %collective-permute-start.2 = (bf16[256,1792]{1,0:T(8,128)(2,1)S(1)}, bf16[256,1792]{1,0:T(8,128)(2,1)}, u32[]{:S(2)}, u32[]{:S(2)}) collective-permute-start(bf16[256,1792]{1,0:T(8,128)(2,1)S(1)} %reshape.107.refs_0_), channel_id=1, source_target_pairs={{0,3},{1,0},{2,1},{3,2},{4,7},{5,4},{6,5},{7,6},{8,11},{9,8},{10,9... | collective-permute-start | bytes 2752520 | tf_op jit(solution)/shard_map/ppermute | solution.py:118
  52.0 23.8 %collective-permute-start = (bf16[256,1792]{1,0:T(8,128)(2,1)S(1)}, bf16[256,1792]{1,0:T(8,128)(2,1)}, u32[]{:S(2)}, u32[]{:S(2)}) collective-permute-start(bf16[256,1792]{1,0:T(8,128)(2,1)S(1)} %reshape.107.refs_0_), channel_id=1, source_target_pairs={{0,1},{1,2},{2,3},{3,0},{4,5},{5,6},{6,7},{7,4},{8,9},{9,10},{10,1... | collective-permute-start | bytes 2752520 | tf_op jit(solution)/shard_map/ppermute | solution.py:118
  52.0 25.0 %copy-start.15 = (s32[4]{0:T(128)S(1)}, s32[4]{0:T(128)}, u32[]{:S(2)}) copy-start(s32[4]{0:T(128)} %constant.100.clone) | copy-start | bytes 52
  56.0 73.1 %collective-permute-start.9 = (bf16[256,1792]{1,0:T(8,128)(2,1)}, bf16[256,1792]{1,0:T(8,128)(2,1)S(1)}, u32[]{:S(2)}, u32[]{:S(2)}) collective-permute-start(bf16[256,1792]{1,0:T(8,128)(2,1)} %get-tuple-element.17), channel_id=1, source_target_pairs={{0,3},{1,0},{2,1},{3,2},{4,7},{5,4},{6,5},{7,6},{8,11},{9,8},{10,9... | collective-permute-start | bytes 2752520 | tf_op jit(solution)/shard_map/ppermute | solution.py:118
  58.6 71.1 %collective-permute-start.7 = (bf16[256,1792]{1,0:T(8,128)(2,1)}, bf16[256,1792]{1,0:T(8,128)(2,1)S(1)}, u32[]{:S(2)}, u32[]{:S(2)}) collective-permute-start(bf16[256,1792]{1,0:T(8,128)(2,1)} %get-tuple-element.18), channel_id=1, source_target_pairs={{0,1},{1,2},{2,3},{3,0},{4,5},{5,6},{6,7},{7,4},{8,9},{9,10},{10,1... | collective-permute-start | bytes 2752520 | tf_op jit(solution)/shard_map/ppermute | solution.py:118
  58.6 71.1 %collective-permute-start.8 = (bf16[256,1792]{1,0:T(8,128)(2,1)}, bf16[256,1792]{1,0:T(8,128)(2,1)}, u32[]{:S(2)}, u32[]{:S(2)}) collective-permute-start(bf16[256,1792]{1,0:T(8,128)(2,1)} %get-tuple-element.20), channel_id=1, source_target_pairs={{0,2},{1,3},{2,0},{3,1},{4,6},{5,7},{6,4},{7,5},{8,10},{9,11},{10,... | collective-permute-start | bytes 2752520 | tf_op jit(solution)/shard_map/ppermute | solution.py:118
  72.3 48.1 %collective-permute-start.3 = (bf16[128,1792]{1,0:T(8,128)(2,1)S(1)}, bf16[128,1792]{1,0:T(8,128)(2,1)}, u32[]{:S(2)}, u32[]{:S(2)}) collective-permute-start(bf16[128,1792]{1,0:T(8,128)(2,1)S(1)} %slice.42), channel_id=1, source_target_pairs={{0,3},{1,0},{2,1},{3,2},{4,7},{5,4},{6,5},{7,6},{8,11},{9,8},{10,9... | collective-permute-start | bytes 1376264 | tf_op jit(solution)/shard_map/ppermute | solution.py:118
  76.9 46.6 %collective-permute-start.1 = (bf16[128,1792]{1,0:T(8,128)(2,1)S(1)}, bf16[128,1792]{1,0:T(8,128)(2,1)S(1)}, u32[]{:S(2)}, u32[]{:S(2)}) collective-permute-start(bf16[128,1792]{1,0:T(8,128)(2,1)S(1)} %slice.41), channel_id=1, source_target_pairs={{0,1},{1,2},{2,3},{3,0},{4,5},{5,6},{6,7},{7,4},{8,9},{9,10},{10,1... | collective-permute-start | bytes 1376264 | tf_op jit(solution)/shard_map/ppermute | solution.py:118
  128.1 4.0 %collective-permute-start.6 = (bf16[256,256]{1,0:T(8,128)(2,1)}, bf16[256,256]{1,0:T(8,128)(2,1)S(1)}, u32[]{:S(2)}, u32[]{:S(2)}) collective-permute-start(bf16[256,256]{1,0:T(8,128)(2,1)} %shard_map.74.refs_0_), channel_id=1, source_target_pairs={{0,3},{1,0},{2,1},{3,2},{4,7},{5,4},{6,5},{7,6},{8,11},{9,8},{10,9... | collective-permute-start | bytes 393224 | tf_op jit(solution)/shard_map/ppermute | solution.py:118
  128.5 5.6 %collective-permute-start.5 = (bf16[256,256]{1,0:T(8,128)(2,1)}, bf16[256,256]{1,0:T(8,128)(2,1)S(1)}, u32[]{:S(2)}, u32[]{:S(2)}) collective-permute-start(bf16[256,256]{1,0:T(8,128)(2,1)} %shard_map.74.refs_0_), channel_id=1, source_target_pairs={{0,2},{1,3},{2,0},{3,1},{4,6},{5,7},{6,4},{7,5},{8,10},{9,11},{10,... | collective-permute-start | bytes 393224 | tf_op jit(solution)/shard_map/ppermute | solution.py:118
  129.1 8.0 %copy-start.3 = (bf16[256,1792]{1,0:T(8,128)(2,1)}, bf16[256,1792]{1,0:T(8,128)(2,1)S(1)}, u32[]{:S(2)}) copy-start(bf16[256,1792]{1,0:T(8,128)(2,1)S(1)} %collective-permute-done.9.refs_7_) | copy-start | bytes 2752516
  129.1 8.0 %collective-permute-start.4 = (bf16[256,256]{1,0:T(8,128)(2,1)}, bf16[256,256]{1,0:T(8,128)(2,1)S(1)}, u32[]{:S(2)}, u32[]{:S(2)}) collective-permute-start(bf16[256,256]{1,0:T(8,128)(2,1)} %shard_map.74.refs_0_), channel_id=1, source_target_pairs={{0,1},{1,2},{2,3},{3,0},{4,5},{5,6},{6,7},{7,4},{8,9},{9,10},{10,1... | collective-permute-start | bytes 393224 | tf_op jit(solution)/shard_map/ppermute | solution.py:118
  129.7 7.3 %copy-start.4 = (bf16[256,1792]{1,0:T(8,128)(2,1)}, bf16[256,1792]{1,0:T(8,128)(2,1)S(1)}, u32[]{:S(2)}) copy-start(bf16[256,1792]{1,0:T(8,128)(2,1)S(1)} %collective-permute-done.7.refs_5_) | copy-start | bytes 2752516
  132.2 4.8 %copy-start.8 = (bf16[256,256]{1,0:T(8,128)(2,1)}, bf16[256,256]{1,0:T(8,128)(2,1)S(1)}, u32[]{:S(2)}) copy-start(bf16[256,256]{1,0:T(8,128)(2,1)S(1)} %collective-permute-done.6.refs_3_) | copy-start | bytes 393220
  134.2 2.9 %copy-start.9 = (bf16[256,256]{1,0:T(8,128)(2,1)}, bf16[256,256]{1,0:T(8,128)(2,1)S(1)}, u32[]{:S(2)}) copy-start(bf16[256,256]{1,0:T(8,128)(2,1)S(1)} %collective-permute-done.5.refs_2_) | copy-start | bytes 393220
  142.3 67.0 %all-to-all-start.1 = ((bf16[64,4,1792]{2,1,0:T(4,128)(2,1)}), bf16[64,4,1792]{2,1,0:T(4,128)(2,1)S(1)}, u32[]{:S(2)}, u32[]{:S(2)}) async-start(bf16[64,4,1792]{2,1,0:T(4,128)(2,1)} %down.2), calls=%async_computation.1 | async-start | bytes 1835008 | tf_op jit(solution)/shard_map/all_to_all | solution.py:121
  156.0 25.2 %copy-start.2 = (bf16[256,1792]{1,0:T(8,128)(2,1)}, bf16[256,1792]{1,0:T(8,128)(2,1)S(1)}, u32[]{:S(2)}) copy-start(bf16[256,1792]{1,0:T(8,128)(2,1)S(1)} %reshape.110.refs_0_) | copy-start | bytes 2752516
  156.0 21.5 %collective-permute-start.12 = (bf16[256,1792]{1,0:T(8,128)(2,1)S(1)}, bf16[256,1792]{1,0:T(8,128)(2,1)S(1)}, u32[]{:S(2)}, u32[]{:S(2)}) collective-permute-start(bf16[256,1792]{1,0:T(8,128)(2,1)S(1)} %reshape.110.refs_0_), channel_id=1, source_target_pairs={{0,3},{1,0},{2,1},{3,2},{4,7},{5,4},{6,5},{7,6},{8,11},{9,8},{10,9... | collective-permute-start | bytes 2752520 | tf_op jit(solution)/shard_map/ppermute | solution.py:118
  156.7 22.8 %collective-permute-start.10 = (bf16[256,1792]{1,0:T(8,128)(2,1)S(1)}, bf16[256,1792]{1,0:T(8,128)(2,1)S(1)}, u32[]{:S(2)}, u32[]{:S(2)}) collective-permute-start(bf16[256,1792]{1,0:T(8,128)(2,1)S(1)} %reshape.110.refs_0_), channel_id=1, source_target_pairs={{0,1},{1,2},{2,3},{3,0},{4,5},{5,6},{6,7},{7,4},{8,9},{9,10},{10,1... | collective-permute-start | bytes 2752520 | tf_op jit(solution)/shard_map/ppermute | solution.py:118
  177.5 3.7 %copy-start.5 = (bf16[256,1792]{1,0:T(8,128)(2,1)}, bf16[256,1792]{1,0:T(8,128)(2,1)S(1)}, u32[]{:S(2)}) copy-start(bf16[256,1792]{1,0:T(8,128)(2,1)S(1)} %collective-permute-done.12.refs_2_) | copy-start | bytes 2752516
  177.6 11.0 %collective-permute-start.13 = (bf16[128,1792]{1,0:T(8,128)(2,1)S(1)}, bf16[128,1792]{1,0:T(8,128)(2,1)}, u32[]{:S(2)}, u32[]{:S(2)}) collective-permute-start(bf16[128,1792]{1,0:T(8,128)(2,1)S(1)} %slice.46), channel_id=1, source_target_pairs={{0,3},{1,0},{2,1},{3,2},{4,7},{5,4},{6,5},{7,6},{8,11},{9,8},{10,9... | collective-permute-start | bytes 1376264 | tf_op jit(solution)/shard_map/ppermute | solution.py:118
  181.2 12.0 %collective-permute-start.11 = (bf16[128,1792]{1,0:T(8,128)(2,1)}, bf16[128,1792]{1,0:T(8,128)(2,1)}, u32[]{:S(2)}, u32[]{:S(2)}) collective-permute-start(bf16[128,1792]{1,0:T(8,128)(2,1)} %slice.45), channel_id=1, source_target_pairs={{0,1},{1,2},{2,3},{3,0},{4,5},{5,6},{6,7},{7,4},{8,9},{9,10},{10,1... | collective-permute-start | bytes 1376264 | tf_op jit(solution)/shard_map/ppermute | solution.py:118
  197.1 26.4 %copy-start.14 = (f32[32,8]{0,1:T(8,128)S(1)}, f32[32,8]{0,1:T(8,128)}, u32[]{:S(2)}) copy-start(f32[32,8]{0,1:T(8,128)} %param.9) | copy-start | bytes 3076
  197.1 4.0 %collective-permute-start.16 = (bf16[256,256]{1,0:T(8,128)(2,1)}, bf16[256,256]{1,0:T(8,128)(2,1)S(1)}, u32[]{:S(2)}, u32[]{:S(2)}) collective-permute-start(bf16[256,256]{1,0:T(8,128)(2,1)} %shard_map.76.refs_0_), channel_id=1, source_target_pairs={{0,3},{1,0},{2,1},{3,2},{4,7},{5,4},{6,5},{7,6},{8,11},{9,8},{10,9... | collective-permute-start | bytes 393224 | tf_op jit(solution)/shard_map/ppermute | solution.py:118
  197.1 5.6 %collective-permute-start.15 = (bf16[256,256]{1,0:T(8,128)(2,1)}, bf16[256,256]{1,0:T(8,128)(2,1)S(1)}, u32[]{:S(2)}, u32[]{:S(2)}) collective-permute-start(bf16[256,256]{1,0:T(8,128)(2,1)} %shard_map.76.refs_0_), channel_id=1, source_target_pairs={{0,2},{1,3},{2,0},{3,1},{4,6},{5,7},{6,4},{7,5},{8,10},{9,11},{10,... | collective-permute-start | bytes 393224 | tf_op jit(solution)/shard_map/ppermute | solution.py:118
  197.9 6.1 %collective-permute-start.14 = (bf16[256,256]{1,0:T(8,128)(2,1)}, bf16[256,256]{1,0:T(8,128)(2,1)S(1)}, u32[]{:S(2)}, u32[]{:S(2)}) collective-permute-start(bf16[256,256]{1,0:T(8,128)(2,1)} %shard_map.76.refs_0_), channel_id=1, source_target_pairs={{0,1},{1,2},{2,3},{3,0},{4,5},{5,6},{6,7},{7,4},{8,9},{9,10},{10,1... | collective-permute-start | bytes 393224 | tf_op jit(solution)/shard_map/ppermute | solution.py:118
  201.1 2.9 %copy-start.10 = (bf16[256,256]{1,0:T(8,128)(2,1)}, bf16[256,256]{1,0:T(8,128)(2,1)S(1)}, u32[]{:S(2)}) copy-start(bf16[256,256]{1,0:T(8,128)(2,1)S(1)} %collective-permute-done.16.refs_3_) | copy-start | bytes 393220
  209.3 39.9 %all-to-all-start.3 = ((bf16[64,4,1792]{2,1,0:T(4,128)(2,1)}), bf16[64,4,1792]{2,1,0:T(4,128)(2,1)S(1)}, u32[]{:S(2)}, u32[]{:S(2)}) async-start(bf16[64,4,1792]{2,1,0:T(4,128)(2,1)} %down.3), calls=%async_computation.3 | async-start | bytes 1835008 | tf_op jit(solution)/shard_map/all_to_all | solution.py:121
  (5 other events, 4.4 us)

commit v4 on v3

--- a/solution.py
+++ b/solution.py
@@ -17,8 +17,30 @@
     return pl.BlockSpec(memory_space=pltpu.VMEM)
 
 
+def land_kernel(blocks, *outs):
+    experts, share, width = blocks.shape
+    half = experts // 2
+    for i, out in enumerate(outs):
+        part = blocks[i * half : (i + 1) * half].astype(F32)
+        out[...] = part.reshape(half * share, width).astype(BF16)
+
+
+def land_of(blocks):
+    experts, share, width = blocks.shape
+    rows, cols = experts * share // 2, width // 2
+    return pl.pallas_call(
+        land_kernel,
+        grid=(2,),
+        in_specs=[pl.BlockSpec((experts, share, cols), lambda k: (0, 0, k))],
+        out_specs=[pl.BlockSpec((rows, cols), lambda k: (0, k))] * 2,
+        out_shape=[jax.ShapeDtypeStruct((rows, width), BF16)] * 2,
+        cost_estimate=pl.CostEstimate(flops=10**7, bytes_accessed=8 * rows * width, transcendentals=0),
+        name="land",
+    )(blocks)
+
+
 def begin_kernel(order_ref, *refs):
-    blocks, (gate_ref, up_ref, gate_acc, up_acc) = refs[:3], refs[3:]
+    blocks, (gate_ref, up_ref, gate_acc, up_acc) = refs[:6], refs[6:]
     step = pl.program_id(0)
 
     @pl.when(step == 0)
@@ -26,12 +48,13 @@
         gate_acc[...] = jnp.zeros_like(gate_acc)
         up_acc[...] = jnp.zeros_like(up_acc)
 
-    for i, block in enumerate(blocks):
+    for i in range(3):
 
         @pl.when(step == i)
-        def _(block=block):
-            gate_acc[...] += jnp.dot(block[...], gate_ref[...], preferred_element_type=F32)
-            up_acc[...] += jnp.dot(block[...], up_ref[...], preferred_element_type=F32)
+        def _(i=i):
+            block = jnp.concatenate([blocks[2 * i][...], blocks[2 * i + 1][...]])
+            gate_acc[...] += jnp.dot(block, gate_ref[...], preferred_element_type=F32)
+            up_acc[...] += jnp.dot(block, up_ref[...], preferred_element_type=F32)
 
 
 def finish_kernel(order_ref, front, rear, gate_ref, up_ref, gate_acc, up_acc, out_ref):
@@ -44,7 +67,7 @@
 
 
 def hidden_of(order, blocks, gate_proj, up_proj):
-    rows, depth = blocks[0].shape
+    rows, depth = 2 * blocks[0].shape[0], blocks[0].shape[1]
     cols = gate_proj.shape[2]
     acc = pl.BlockSpec((rows, cols), lambda k, order: (0, 0))
 
@@ -68,8 +91,8 @@
             ),
         )(order, *given, gate_proj, up_proj, *more)
 
-    partial = call(begin_kernel, 0, 3, blocks[:3], [], [F32, F32])
-    return call(finish_kernel, 3, 1, blocks[3:], partial, [BF16])[0]
+    partial = call(begin_kernel, 0, 3, blocks[:6], [], [F32, F32])
+    return call(finish_kernel, 3, 1, blocks[6:], partial, [BF16])[0]
 
 
 def down_kernel(pairs, *refs):
@@ -120,11 +143,10 @@
     def exchange(blocks):
         return lax.all_to_all(blocks, "ep", split_axis=0, concat_axis=0, tiled=True)
 
-    downs = []
-    for by in range(parts):
-        start = (tp + by) % parts * width
-        piece = lax.dynamic_slice_in_dim(w_down, start, width, axis=1)
-        downs.append(piece if by == 0 else over_y(piece, by))
+    def piece(source, by):
+        return lax.dynamic_slice_in_dim(source, (tp + by) % parts * width, width, axis=1)
+
+    after, before_it = over_y(piece(w_down, 1), 1), over_y(piece(w_down, -1), -1)
 
     flat_ids = routes.reshape(-1)
     onehot = (flat_ids[:, None] == jnp.arange(experts, dtype=jnp.int32)[None, :]).astype(jnp.int32)
@@ -132,7 +154,7 @@
     position = jnp.sum(before * onehot, axis=1)
     target = (flat_ids * capacity + position).reshape(tok_count, fanout)
 
-    mixed = jnp.zeros((tok_count, width), F32)
+    selections = []
     first = 0
     for size in SIZES:
         row = jnp.arange(experts * size, dtype=jnp.int32)
@@ -140,15 +162,24 @@
         first += size
         select = jnp.any(target[None, :, :] == slot[:, None, None], axis=2).astype(BF16)
         sending = jnp.dot(select, tokens, preferred_element_type=F32).astype(BF16)
-        landed = exchange(sending.reshape(experts, size, width))
-        mine = landed.reshape(-1, width)
-        cut = mine.shape[0] // 2
-        left = over_y(mine, 1)
-        right = over_y(mine, -1)
-        left_cut, right_cut = left[:cut], right[cut:]
-        front = over_y(left_cut, 1)
-        rear = over_y(right_cut, -1)
-        hidden = hidden_of(order, [mine, left, right, front, rear], gate_proj, up_proj)
+        selections.append((slot, sending.reshape(experts, size, width)))
+
+    w_late, last_sending = lax.optimization_barrier((w_down, selections[-1][1]))
+    selections[-1] = (selections[-1][0], last_sending)
+    opposite = over_y(piece(w_late, 2), 2)
+    downs = [piece(w_late, 0), after, opposite, before_it]
+
+    mixed = jnp.zeros((tok_count, width), F32)
+    for slot, sending in selections:
+        landed = exchange(sending)
+        mine = land_of(landed)
+        left = [over_y(mine[0], 1)]
+        right = [over_y(mine[1], -1)]
+        left.append(over_y(mine[1], 1))
+        right.insert(0, over_y(mine[0], -1))
+        front = over_y(left[0], 1)
+        rear = over_y(right[1], -1)
+        hidden = hidden_of(order, [*mine, *left, *right, front, rear], gate_proj, up_proj)
         hiddens = [hidden] + [over_y(hidden, by) for by in range(1, parts)]
         out = down_of(hiddens, downs, experts)
         back = exchange(out).reshape(-1, width)

time: 251 us -> 250 us (level)
  waiting for transfers between devices: 138 us -> 128 us
  starting transfers between devices: 62.4 us -> 67.6 us
  Pallas kernels: 30.1 us -> 34.1 us
    ppermute x17 -> x21, waiting for transfers between devices: 89 us -> 79 us  [over_y(): lax.ppermute(value, 'tp', [(i, (i + by) % parts) for i in range(parts)])]
    ppermute x17 -> x21, starting transfers between devices: 16.9 us -> 23.4 us  [over_y(): lax.ppermute(value, 'tp', [(i, (i + by) % parts) for i in range(parts)])]
    pallas_call x0 -> x2, Pallas kernels: none -> 4.06 us  [land_of(): pl.pallas_call(land_kernel, grid=(2,), in_specs=[pl.BlockSpec((experts, s...]
    unnamed x34 -> x48, local copies, waits for them, and re-layouts: 3.9 us -> 6.97 us
    slice x5 -> x1, local copies, waits for them, and re-layouts: 3.15 us -> 0.18 us  [the longest x4 2.96 us: layer(): left_cut, right_cut = (left[:cut], right[cut:])]
    dynamic_slice x1 -> x2, local copies, waits for them, and re-layouts: 3.9 us -> 5.68 us  [piece(): lax.dynamic_slice_in_dim(source, (tp + by) % parts * width, width, axis=1)]
  transfers between devices with their start and end apart: 21 -> 25, of which waited for: 14 -> 15; matrix products, arithmetic and copies ran while one was open for 5% -> 3% of each run, Pallas kernels for 12% -> 14%
where the time goes in v4:
time: 250 us
  waiting for transfers between devices  128 us (51%)
  starting transfers between devices  67.6 us (27%)
  Pallas kernels  34.1 us (14%)
  local copies, waits for them, and re-layouts  15.8 us (6%)
    ppermute x21, waiting for transfers between devices, over_y(): lax.ppermute(value, 'tp', [(i, (i + by) % parts) for i in range(parts)])  79 us
    all_to_all x4, waiting for transfers between devices, exchange(): return lax.all_to_all(blocks, 'ep', split_axis=0, concat_axis=0, tiled=True)  49 us
    all_to_all x4, starting transfers between devices, exchange(): return lax.all_to_all(blocks, 'ep', split_axis=0, concat_axis=0, tiled=True)  44.2 us
    ppermute x21, starting transfers between devices, over_y(): lax.ppermute(value, 'tp', [(i, (i + by) % parts) for i in range(parts)])  23.4 us
    pallas_call x4, Pallas kernels, call(): pl.pallas_call(kernel, grid_spec=pltpu.PrefetchScalarGridSpec(num_scalar_...  20.8 us
    pallas_call x2, Pallas kernels, down_of(): pl.pallas_call(functools.partial(down_kernel, n), in_specs=[vmem()] * (2...  9.28 us
    unnamed x48, local copies, waits for them, and re-layouts  6.97 us
    dynamic_slice x2, local copies, waits for them, and re-layouts, piece(): lax.dynamic_slice_in_dim(source, (tp + by) % parts * width, width, axis=1)  5.68 us
  transfers between devices with their start and end apart: 25, of which 15 were waited for; matrix products, arithmetic and copies ran while one was open for 3% of the time, Pallas kernels for 14%

profile of v4, /device:TPU:1, one launch (start us, length us, event | category | flops | bytes accessed | tf_op | source)
XLA Modules:
  0.0 249.7 jit_solution(6829523004121017543)
XLA Ops:
  3.9 13.0 %all-to-all-start = ((bf16[64,4,1792]{2,1,0:T(4,128)(2,1)}), bf16[64,4,1792]{2,1,0:T(4,128)(2,1)S(1)}, u32[]{:S(2)}, u32[]{:S(2)}) async-start(bf16[64,4,1792]{2,1,0:T(4,128)(2,1)} %reshape.98), calls=%async_computation | async-start | bytes 1835008 | tf_op jit(solution)/shard_map/all_to_all | solution.py:144
  18.5 24.1 %all-to-all-done.blocks = bf16[64,4,1792]{2,1,0:T(4,128)(2,1)S(1)} async-done(((bf16[64,4,1792]{2,1,0:T(4,128)(2,1)}), bf16[64,4,1792]{2,1,0:T(4,128)(2,1)S(1)}, u32[]{:S(2)}, u32[]{:S(2)}) %all-to-all-start) | async-done | bytes 917536 | tf_op jit(solution)/shard_map/all_to_all | solution.py:144
  42.6 6.4 %all-to-all-start.2 = ((bf16[64,4,1792]{2,1,0:T(4,128)(2,1)}), bf16[64,4,1792]{2,1,0:T(4,128)(2,1)}, u32[]{:S(2)}, u32[]{:S(2)}) async-start(bf16[64,4,1792]{2,1,0:T(4,128)(2,1)} %reshape.99), calls=%async_computation.2 | async-start | bytes 1835008 | tf_op jit(solution)/shard_map/all_to_all | solution.py:144
  49.0 2.0 land.2
  51.1 2.8 %collective-permute-start.5 = (bf16[128,1792]{1,0:T(8,128)(2,1)}, bf16[128,1792]{1,0:T(8,128)(2,1)S(1)}, u32[]{:S(2)}, u32[]{:S(2)}) collective-permute-start(bf16[128,1792]{1,0:T(8,128)(2,1)} %get-tuple-element.15.refs_0_), channel_id=1, source_target_pairs={{0,3},{1,0},{2,1},{3,2},{4,7},{5,4},{6,5},{7,6},{8,11},{9,8},{10,9... | collective-permute-start | bytes 1376264 | tf_op jit(solution)/shard_map/ppermute | solution.py:141
  53.9 2.8 %constant_dynamic-slice_fusion = (bf16[256,1792]{1,0:T(8,128)(2,1)}, bf16[256,1792]{1,0:T(8,128)(2,1)}) fusion(bf16[256,7168]{1,0:T(8,128)(2,1)} %bitcast.30, s32[]{:T(128)S(6)} %select_n.107, s32[]{:T(128)S(6)} %select_n.103), kind=kLoop, calls=%fused_computation.48 | loop fusion | bytes 3670024 | tf_op jit(solution)/shard_map/dynamic_slice | solution.py:147
  61.0 2.8 %dynamic-slice_bitcast_fusion = (bf16[256,1792]{1,0:T(8,128)(2,1)}, bf16[256,1792]{1,0:T(8,128)(2,1)}) fusion(bf16[1,256,7168]{2,1,0:T(8,128)(2,1)} %param.12, s32[]{:T(128)S(6)} %select_n.109, s32[]{:T(128)S(6)} %select_n.105), kind=kLoop, calls=%fused_computation.2 | loop fusion | bytes 3670024 | tf_op jit(solution)/shard_map/dynamic_slice | solution.py:147
  63.9 18.4 %collective-permute-done.5.refs_4_ = bf16[128,1792]{1,0:T(8,128)(2,1)S(1)} collective-permute-done((bf16[128,1792]{1,0:T(8,128)(2,1)}, bf16[128,1792]{1,0:T(8,128)(2,1)S(1)}, u32[]{:S(2)}, u32[]{:S(2)}) %collective-permute-start.5) | collective-permute-done | bytes 458784 | tf_op jit(solution)/shard_map/ppermute | solution.py:141
  83.0 3.8 %collective-permute-start.11 = (bf16[256,1792]{1,0:T(8,128)(2,1)}, bf16[256,1792]{1,0:T(8,128)(2,1)S(1)}, u32[]{:S(2)}, u32[]{:S(2)}) collective-permute-start(bf16[256,1792]{1,0:T(8,128)(2,1)} %get-tuple-element.29), channel_id=1, source_target_pairs={{0,3},{1,0},{2,1},{3,2},{4,7},{5,4},{6,5},{7,6},{8,11},{9,8},{10,9... | collective-permute-start | bytes 2752520 | tf_op jit(solution)/shard_map/ppermute | solution.py:141
  87.7 8.4 %collective-permute-done.4.refs_3_ = bf16[128,1792]{1,0:T(8,128)(2,1)S(1)} collective-permute-done((bf16[128,1792]{1,0:T(8,128)(2,1)S(1)}, bf16[128,1792]{1,0:T(8,128)(2,1)S(1)}, u32[]{:S(2)}, u32[]{:S(2)}) %collective-permute-start.4) | collective-permute-done | bytes 458784 | tf_op jit(solution)/shard_map/ppermute | solution.py:141
  96.9 1.9 collective-permute-start.3
  99.2 6.5 %shard_map.73 = (f32[256,256]{1,0:T(8,128)}, f32[256,256]{1,0:T(8,128)}) custom-call(s32[4]{0:T(128)} %and_select_fusion.order_ref, bf16[128,1792]{1,0:T(8,128)(2,1)} %get-tuple-element.15.refs_0_, bf16[128,1792]{1,0:T(8,128)(2,1)} %get-tuple-element.16.refs_1_, bf16[128,1792]{1,0:T(8,128)(2,1)} %copy-done.7, bf16[128,1792]{1,0:T(8,128)(2,1)} %copy-done.8, ...), custom_call_target="tpu_custom_call" | custom-call | flops 1409286144 | bytes 8257536 | tf_op jit(solution)/shard_map/pallas_call | solution.py:76
  105.8 19.9 %collective-permute-done.1.front = bf16[128,1792]{1,0:T(8,128)(2,1)} collective-permute-done((bf16[128,1792]{1,0:T(8,128)(2,1)}, bf16[128,1792]{1,0:T(8,128)(2,1)}, u32[]{:S(2)}, u32[]{:S(2)}) %collective-permute-start.1) | collective-permute-done | bytes 458784 | tf_op jit(solution)/shard_map/ppermute | solution.py:141
  126.4 3.8 %shard_map.74.refs_0_ = bf16[256,256]{1,0:T(8,128)(2,1)} custom-call(s32[4]{0:T(128)} %and_select_fusion.order_ref, bf16[128,1792]{1,0:T(8,128)(2,1)} %collective-permute-done.1.front, bf16[128,1792]{1,0:T(8,128)(2,1)} %copy-done.14, bf16[1,7168,256]{2,1,0:T(8,128)(2,1)} %gate_ref.3, bf16[1,7168,256]{2,1,0:T(8,128)(2,1)} %up_ref.3, ...), custom_call_target="tpu_custom_call" | custom-call | flops 469762048 | bytes 2752512 | tf_op jit(solution)/shard_map/pallas_call | solution.py:76
  131.8 2.5 collective-permute-done.8.refs_3_
  136.0 2.7 %collective-permute-done.6.refs_1_ = bf16[256,256]{1,0:T(8,128)(2,1)S(1)} collective-permute-done((bf16[256,256]{1,0:T(8,128)(2,1)}, bf16[256,256]{1,0:T(8,128)(2,1)S(1)}, u32[]{:S(2)}, u32[]{:S(2)}) %collective-permute-start.6) | collective-permute-done | bytes 131104 | tf_op jit(solution)/shard_map/ppermute | solution.py:141
  139.3 4.7 %down.2 = bf16[64,4,1792]{2,1,0:T(4,128)(2,1)} custom-call(bf16[256,256]{1,0:T(8,128)(2,1)} %shard_map.74.refs_0_, bf16[256,256]{1,0:T(8,128)(2,1)} %copy-done.18, bf16[256,256]{1,0:T(8,128)(2,1)} %copy-done.16, bf16[256,256]{1,0:T(8,128)(2,1)} %copy-done.15, bf16[256,1792]{1,0:T(8,128)(2,1)} %get-tuple-element.32.refs_4_, bf16[256,1792]{1,0:T(8,128)(2,1)} %copy-done.3, ...), custom_call_target="tpu_custom_call" | custom-call | flops 939524096 | bytes 5111808 | tf_op jit(solution)/shard_map/down/pallas_call | solution.py:116
  144.0 12.2 %all-to-all-start.1 = ((bf16[64,4,1792]{2,1,0:T(4,128)(2,1)}), bf16[64,4,1792]{2,1,0:T(4,128)(2,1)S(1)}, u32[]{:S(2)}, u32[]{:S(2)}) async-start(bf16[64,4,1792]{2,1,0:T(4,128)(2,1)} %down.2), calls=%async_computation.1 | async-start | bytes 1835008 | tf_op jit(solution)/shard_map/all_to_all | solution.py:144
  156.2 2.0 land.3
  158.3 2.7 %collective-permute-start.14 = (bf16[128,1792]{1,0:T(8,128)(2,1)}, bf16[128,1792]{1,0:T(8,128)(2,1)S(1)}, u32[]{:S(2)}, u32[]{:S(2)}) collective-permute-start(bf16[128,1792]{1,0:T(8,128)(2,1)} %get-tuple-element.22.refs_1_), channel_id=1, source_target_pairs={{0,3},{1,0},{2,1},{3,2},{4,7},{5,4},{6,5},{7,6},{8,11},{9,8},{10,9... | collective-permute-start | bytes 1376264 | tf_op jit(solution)/shard_map/ppermute | solution.py:141
  162.4 8.9 %collective-permute-done.12.refs_2_ = bf16[128,1792]{1,0:T(8,128)(2,1)S(1)} collective-permute-done((bf16[128,1792]{1,0:T(8,128)(2,1)}, bf16[128,1792]{1,0:T(8,128)(2,1)S(1)}, u32[]{:S(2)}, u32[]{:S(2)}) %collective-permute-start.12) | collective-permute-done | bytes 458784 | tf_op jit(solution)/shard_map/ppermute | solution.py:141
  171.3 2.7 %collective-permute-start.15 = (bf16[128,1792]{1,0:T(8,128)(2,1)S(1)}, bf16[128,1792]{1,0:T(8,128)(2,1)}, u32[]{:S(2)}, u32[]{:S(2)}) collective-permute-start(bf16[128,1792]{1,0:T(8,128)(2,1)S(1)} %collective-permute-done.14.refs_5_), channel_id=1, source_target_pairs={{0,3},{1,0},{2,1},{3,2},{4,7},{5,4},{6,5},{7,6},{8,11},{9,8},{10,9... | collective-permute-start | bytes 1376264 | tf_op jit(solution)/shard_map/ppermute | solution.py:141
  174.0 6.2 %collective-permute-done.17.refs_4_ = bf16[128,1792]{1,0:T(8,128)(2,1)S(1)} collective-permute-done((bf16[128,1792]{1,0:T(8,128)(2,1)}, bf16[128,1792]{1,0:T(8,128)(2,1)S(1)}, u32[]{:S(2)}, u32[]{:S(2)}) %collective-permute-start.17) | collective-permute-done | bytes 458784 | tf_op jit(solution)/shard_map/ppermute | solution.py:141
  181.9 6.6 %shard_map.75 = (f32[256,256]{1,0:T(8,128)}, f32[256,256]{1,0:T(8,128)}) custom-call(s32[4]{0:T(128)} %and_select_fusion.order_ref, bf16[128,1792]{1,0:T(8,128)(2,1)} %get-tuple-element.21.refs_0_, bf16[128,1792]{1,0:T(8,128)(2,1)} %get-tuple-element.22.refs_1_, bf16[128,1792]{1,0:T(8,128)(2,1)} %copy-done.9, bf16[128,1792]{1,0:T(8,128)(2,1)} %copy-done.13, ...), custom_call_target="tpu_custom_call" | custom-call | flops 1409286144 | bytes 8257536 | tf_op jit(solution)/shard_map/pallas_call | solution.py:76
  188.5 2.5 %collective-permute-done.13.front = bf16[128,1792]{1,0:T(8,128)(2,1)S(1)} collective-permute-done((bf16[128,1792]{1,0:T(8,128)(2,1)S(1)}, bf16[128,1792]{1,0:T(8,128)(2,1)S(1)}, u32[]{:S(2)}, u32[]{:S(2)}) %collective-permute-start.13) | collective-permute-done | bytes 458784 | tf_op jit(solution)/shard_map/ppermute | solution.py:141
  191.8 3.8 %shard_map.76.refs_0_ = bf16[256,256]{1,0:T(8,128)(2,1)} custom-call(s32[4]{0:T(128)} %and_select_fusion.order_ref, bf16[128,1792]{1,0:T(8,128)(2,1)} %copy-done.11, bf16[128,1792]{1,0:T(8,128)(2,1)} %collective-permute-done.15.rear, bf16[1,7168,256]{2,1,0:T(8,128)(2,1)} %gate_ref.3, bf16[1,7168,256]{2,1,0:T(8,128)(2,1)} %up_ref.3, ...), custom_call_target="tpu_custom_call" | custom-call | flops 469762048 | bytes 2752512 | tf_op jit(solution)/shard_map/pallas_call | solution.py:76
  197.9 2.4 collective-permute-done.20.refs_3_
  200.3 2.6 %collective-permute-done.19.refs_2_ = bf16[256,256]{1,0:T(8,128)(2,1)S(1)} collective-permute-done((bf16[256,256]{1,0:T(8,128)(2,1)}, bf16[256,256]{1,0:T(8,128)(2,1)S(1)}, u32[]{:S(2)}, u32[]{:S(2)}) %collective-permute-start.19) | collective-permute-done | bytes 131104 | tf_op jit(solution)/shard_map/ppermute | solution.py:141
  203.0 1.9 collective-permute-done.18.refs_1_
  205.5 4.6 %down.3 = bf16[64,4,1792]{2,1,0:T(4,128)(2,1)} custom-call(bf16[256,256]{1,0:T(8,128)(2,1)} %shard_map.76.refs_0_, bf16[256,256]{1,0:T(8,128)(2,1)} %copy-done.20, bf16[256,256]{1,0:T(8,128)(2,1)} %copy-done.19, bf16[256,256]{1,0:T(8,128)(2,1)} %copy-done.17, bf16[256,1792]{1,0:T(8,128)(2,1)} %get-tuple-element.32.refs_4_, bf16[256,1792]{1,0:T(8,128)(2,1)} %copy-done.3, ...), custom_call_target="tpu_custom_call" | custom-call | flops 939524096 | bytes 5111808 | tf_op jit(solution)/shard_map/down/pallas_call | solution.py:116
  210.2 12.6 %all-to-all-start.3 = ((bf16[64,4,1792]{2,1,0:T(4,128)(2,1)}), bf16[64,4,1792]{2,1,0:T(4,128)(2,1)S(1)}, u32[]{:S(2)}, u32[]{:S(2)}) async-start(bf16[64,4,1792]{2,1,0:T(4,128)(2,1)} %down.3), calls=%async_computation.3 | async-start | bytes 1835008 | tf_op jit(solution)/shard_map/all_to_all | solution.py:144
  223.6 24.9 %all-to-all-done.3 = bf16[64,4,1792]{2,1,0:T(4,128)(2,1)S(1)} async-done(((bf16[64,4,1792]{2,1,0:T(4,128)(2,1)}), bf16[64,4,1792]{2,1,0:T(4,128)(2,1)S(1)}, u32[]{:S(2)}, u32[]{:S(2)}) %all-to-all-start.3) | async-done | bytes 917536 | tf_op jit(solution)/shard_map/all_to_all | solution.py:144
  (101 shorter events, 26.4 us)
Async XLA Ops:
  3.9 38.7 %all-to-all-start = ((bf16[64,4,1792]{2,1,0:T(4,128)(2,1)}), bf16[64,4,1792]{2,1,0:T(4,128)(2,1)S(1)}, u32[]{:S(2)}, u32[]{:S(2)}) async-start(bf16[64,4,1792]{2,1,0:T(4,128)(2,1)} %reshape.98), calls=%async_computation | async-start | bytes 1835008 | tf_op jit(solution)/shard_map/all_to_all | solution.py:144
  42.6 101.4 %all-to-all-start.2 = ((bf16[64,4,1792]{2,1,0:T(4,128)(2,1)}), bf16[64,4,1792]{2,1,0:T(4,128)(2,1)}, u32[]{:S(2)}, u32[]{:S(2)}) async-start(bf16[64,4,1792]{2,1,0:T(4,128)(2,1)} %reshape.99), calls=%async_computation.2 | async-start | bytes 1835008 | tf_op jit(solution)/shard_map/all_to_all | solution.py:144
  51.1 7.3 %copy-start.5 = (bf16[128,1792]{1,0:T(8,128)(2,1)S(1)}, bf16[128,1792]{1,0:T(8,128)(2,1)}, u32[]{:S(2)}) copy-start(bf16[128,1792]{1,0:T(8,128)(2,1)} %get-tuple-element.16.refs_1_) | copy-start | bytes 1376260
  51.1 47.6 %copy-start.22 = (s32[4]{0:T(128)S(1)}, s32[4]{0:T(128)}, u32[]{:S(2)}) copy-start(s32[4]{0:T(128)} %constant.98.clone) | copy-start | bytes 52
  51.1 31.1 %collective-permute-start.5 = (bf16[128,1792]{1,0:T(8,128)(2,1)}, bf16[128,1792]{1,0:T(8,128)(2,1)S(1)}, u32[]{:S(2)}, u32[]{:S(2)}) collective-permute-start(bf16[128,1792]{1,0:T(8,128)(2,1)} %get-tuple-element.15.refs_0_), channel_id=1, source_target_pairs={{0,3},{1,0},{2,1},{3,2},{4,7},{5,4},{6,5},{7,6},{8,11},{9,8},{10,9... | collective-permute-start | bytes 1376264 | tf_op jit(solution)/shard_map/ppermute | solution.py:141
  53.8 33.0 %collective-permute-start = (bf16[128,1792]{1,0:T(8,128)(2,1)}, bf16[128,1792]{1,0:T(8,128)(2,1)S(1)}, u32[]{:S(2)}, u32[]{:S(2)}) collective-permute-start(bf16[128,1792]{1,0:T(8,128)(2,1)} %get-tuple-element.15.refs_0_), channel_id=1, source_target_pairs={{0,1},{1,2},{2,3},{3,0},{4,5},{5,6},{6,7},{7,4},{8,9},{9,10},{10,1... | collective-permute-start | bytes 1376264 | tf_op jit(solution)/shard_map/ppermute | solution.py:141
  56.7 74.5 %collective-permute-start.10 = (bf16[256,1792]{1,0:T(8,128)(2,1)}, bf16[256,1792]{1,0:T(8,128)(2,1)S(1)}, u32[]{:S(2)}, u32[]{:S(2)}) collective-permute-start(bf16[256,1792]{1,0:T(8,128)(2,1)} %get-tuple-element.31), channel_id=1, source_target_pairs={{0,2},{1,3},{2,0},{3,1},{4,6},{5,7},{6,4},{7,5},{8,10},{9,11},{10,... | collective-permute-start | bytes 2752520 | tf_op jit(solution)/shard_map/ppermute | solution.py:141
  58.3 37.7 %collective-permute-start.4 = (bf16[128,1792]{1,0:T(8,128)(2,1)S(1)}, bf16[128,1792]{1,0:T(8,128)(2,1)S(1)}, u32[]{:S(2)}, u32[]{:S(2)}) collective-permute-start(bf16[128,1792]{1,0:T(8,128)(2,1)S(1)} %copy-done.5), channel_id=1, source_target_pairs={{0,1},{1,2},{2,3},{3,0},{4,5},{5,6},{6,7},{7,4},{8,9},{9,10},{10,1... | collective-permute-start | bytes 1376264 | tf_op jit(solution)/shard_map/ppermute | solution.py:141
  60.0 36.1 %collective-permute-start.2 = (bf16[128,1792]{1,0:T(8,128)(2,1)S(1)}, bf16[128,1792]{1,0:T(8,128)(2,1)}, u32[]{:S(2)}, u32[]{:S(2)}) collective-permute-start(bf16[128,1792]{1,0:T(8,128)(2,1)S(1)} %copy-done.5), channel_id=1, source_target_pairs={{0,3},{1,0},{2,1},{3,2},{4,7},{5,4},{6,5},{7,6},{8,11},{9,8},{10,9... | collective-permute-start | bytes 1376264 | tf_op jit(solution)/shard_map/ppermute | solution.py:141
  83.0 48.8 %collective-permute-start.11 = (bf16[256,1792]{1,0:T(8,128)(2,1)}, bf16[256,1792]{1,0:T(8,128)(2,1)S(1)}, u32[]{:S(2)}, u32[]{:S(2)}) collective-permute-start(bf16[256,1792]{1,0:T(8,128)(2,1)} %get-tuple-element.29), channel_id=1, source_target_pairs={{0,3},{1,0},{2,1},{3,2},{4,7},{5,4},{6,5},{7,6},{8,11},{9,8},{10,9... | collective-permute-start | bytes 2752520 | tf_op jit(solution)/shard_map/ppermute | solution.py:141
  87.7 44.2 %collective-permute-start.9 = (bf16[256,1792]{1,0:T(8,128)(2,1)}, bf16[256,1792]{1,0:T(8,128)(2,1)S(1)}, u32[]{:S(2)}, u32[]{:S(2)}) collective-permute-start(bf16[256,1792]{1,0:T(8,128)(2,1)} %get-tuple-element.30), channel_id=1, source_target_pairs={{0,1},{1,2},{2,3},{3,0},{4,5},{5,6},{6,7},{7,4},{8,9},{9,10},{10,1... | collective-permute-start | bytes 2752520 | tf_op jit(solution)/shard_map/ppermute | solution.py:141
  96.0 29.6 %collective-permute-start.1 = (bf16[128,1792]{1,0:T(8,128)(2,1)}, bf16[128,1792]{1,0:T(8,128)(2,1)}, u32[]{:S(2)}, u32[]{:S(2)}) collective-permute-start(bf16[128,1792]{1,0:T(8,128)(2,1)} %copy-done.7), channel_id=1, source_target_pairs={{0,1},{1,2},{2,3},{3,0},{4,5},{5,6},{6,7},{7,4},{8,9},{9,10},{10,1... | collective-permute-start | bytes 1376264 | tf_op jit(solution)/shard_map/ppermute | solution.py:141
  96.9 28.8 %collective-permute-start.3 = (bf16[128,1792]{1,0:T(8,128)(2,1)}, bf16[128,1792]{1,0:T(8,128)(2,1)S(1)}, u32[]{:S(2)}, u32[]{:S(2)}) collective-permute-start(bf16[128,1792]{1,0:T(8,128)(2,1)} %collective-permute-done.2.refs_5_), channel_id=1, source_target_pairs={{0,3},{1,0},{2,1},{3,2},{4,7},{5,4},{6,5},{7,6},{8,11},{9,8},{10,9... | collective-permute-start | bytes 1376264 | tf_op jit(solution)/shard_map/ppermute | solution.py:141
  130.3 4.0 %collective-permute-start.8 = (bf16[256,256]{1,0:T(8,128)(2,1)}, bf16[256,256]{1,0:T(8,128)(2,1)S(1)}, u32[]{:S(2)}, u32[]{:S(2)}) collective-permute-start(bf16[256,256]{1,0:T(8,128)(2,1)} %shard_map.74.refs_0_), channel_id=1, source_target_pairs={{0,3},{1,0},{2,1},{3,2},{4,7},{5,4},{6,5},{7,6},{8,11},{9,8},{10,9... | collective-permute-start | bytes 393224 | tf_op jit(solution)/shard_map/ppermute | solution.py:141
  130.4 5.6 %collective-permute-start.7 = (bf16[256,256]{1,0:T(8,128)(2,1)}, bf16[256,256]{1,0:T(8,128)(2,1)S(1)}, u32[]{:S(2)}, u32[]{:S(2)}) collective-permute-start(bf16[256,256]{1,0:T(8,128)(2,1)} %shard_map.74.refs_0_), channel_id=1, source_target_pairs={{0,2},{1,3},{2,0},{3,1},{4,6},{5,7},{6,4},{7,5},{8,10},{9,11},{10,... | collective-permute-start | bytes 393224 | tf_op jit(solution)/shard_map/ppermute | solution.py:141
  131.2 7.5 %copy-start.1 = (bf16[256,1792]{1,0:T(8,128)(2,1)}, bf16[256,1792]{1,0:T(8,128)(2,1)S(1)}, u32[]{:S(2)}) copy-start(bf16[256,1792]{1,0:T(8,128)(2,1)S(1)} %collective-permute-done.10.refs_6_) | copy-start | bytes 2752516
  131.2 7.5 %collective-permute-start.6 = (bf16[256,256]{1,0:T(8,128)(2,1)}, bf16[256,256]{1,0:T(8,128)(2,1)S(1)}, u32[]{:S(2)}, u32[]{:S(2)}) collective-permute-start(bf16[256,256]{1,0:T(8,128)(2,1)} %shard_map.74.refs_0_), channel_id=1, source_target_pairs={{0,1},{1,2},{2,3},{3,0},{4,5},{5,6},{6,7},{7,4},{8,9},{9,10},{10,1... | collective-permute-start | bytes 393224 | tf_op jit(solution)/shard_map/ppermute | solution.py:141
  131.8 6.9 %copy-start.2 = (bf16[256,1792]{1,0:T(8,128)(2,1)}, bf16[256,1792]{1,0:T(8,128)(2,1)S(1)}, u32[]{:S(2)}) copy-start(bf16[256,1792]{1,0:T(8,128)(2,1)S(1)} %collective-permute-done.11.refs_7_) | copy-start | bytes 2752516
  144.0 66.2 %all-to-all-start.1 = ((bf16[64,4,1792]{2,1,0:T(4,128)(2,1)}), bf16[64,4,1792]{2,1,0:T(4,128)(2,1)S(1)}, u32[]{:S(2)}, u32[]{:S(2)}) async-start(bf16[64,4,1792]{2,1,0:T(4,128)(2,1)} %down.2), calls=%async_computation.1 | async-start | bytes 1835008 | tf_op jit(solution)/shard_map/all_to_all | solution.py:144
  158.3 13.0 %collective-permute-start.12 = (bf16[128,1792]{1,0:T(8,128)(2,1)}, bf16[128,1792]{1,0:T(8,128)(2,1)S(1)}, u32[]{:S(2)}, u32[]{:S(2)}) collective-permute-start(bf16[128,1792]{1,0:T(8,128)(2,1)} %get-tuple-element.21.refs_0_), channel_id=1, source_target_pairs={{0,1},{1,2},{2,3},{3,0},{4,5},{5,6},{6,7},{7,4},{8,9},{9,10},{10,1... | collective-permute-start | bytes 1376264 | tf_op jit(solution)/shard_map/ppermute | solution.py:141
  158.3 13.1 %collective-permute-start.14 = (bf16[128,1792]{1,0:T(8,128)(2,1)}, bf16[128,1792]{1,0:T(8,128)(2,1)S(1)}, u32[]{:S(2)}, u32[]{:S(2)}) collective-permute-start(bf16[128,1792]{1,0:T(8,128)(2,1)} %get-tuple-element.22.refs_1_), channel_id=1, source_target_pairs={{0,3},{1,0},{2,1},{3,2},{4,7},{5,4},{6,5},{7,6},{8,11},{9,8},{10,9... | collective-permute-start | bytes 1376264 | tf_op jit(solution)/shard_map/ppermute | solution.py:141
  161.0 19.3 %collective-permute-start.17 = (bf16[128,1792]{1,0:T(8,128)(2,1)}, bf16[128,1792]{1,0:T(8,128)(2,1)S(1)}, u32[]{:S(2)}, u32[]{:S(2)}) collective-permute-start(bf16[128,1792]{1,0:T(8,128)(2,1)} %get-tuple-element.21.refs_0_), channel_id=1, source_target_pairs={{0,3},{1,0},{2,1},{3,2},{4,7},{5,4},{6,5},{7,6},{8,11},{9,8},{10,9... | collective-permute-start | bytes 1376264 | tf_op jit(solution)/shard_map/ppermute | solution.py:141
  161.0 20.2 %collective-permute-start.16 = (bf16[128,1792]{1,0:T(8,128)(2,1)}, bf16[128,1792]{1,0:T(8,128)(2,1)S(1)}, u32[]{:S(2)}, u32[]{:S(2)}) collective-permute-start(bf16[128,1792]{1,0:T(8,128)(2,1)} %get-tuple-element.22.refs_1_), channel_id=1, source_target_pairs={{0,1},{1,2},{2,3},{3,0},{4,5},{5,6},{6,7},{7,4},{8,9},{9,10},{10,1... | collective-permute-start | bytes 1376264 | tf_op jit(solution)/shard_map/ppermute | solution.py:141
  171.3 9.8 %copy-start.9 = (bf16[128,1792]{1,0:T(8,128)(2,1)}, bf16[128,1792]{1,0:T(8,128)(2,1)S(1)}, u32[]{:S(2)}) copy-start(bf16[128,1792]{1,0:T(8,128)(2,1)S(1)} %collective-permute-done.12.refs_2_) | copy-start | bytes 1376260
  171.3 19.7 %collective-permute-start.13 = (bf16[128,1792]{1,0:T(8,128)(2,1)S(1)}, bf16[128,1792]{1,0:T(8,128)(2,1)S(1)}, u32[]{:S(2)}, u32[]{:S(2)}) collective-permute-start(bf16[128,1792]{1,0:T(8,128)(2,1)S(1)} %collective-permute-done.12.refs_2_), channel_id=1, source_target_pairs={{0,1},{1,2},{2,3},{3,0},{4,5},{5,6},{6,7},{7,4},{8,9},{9,10},{10,1... | collective-permute-start | bytes 1376264 | tf_op jit(solution)/shard_map/ppermute | solution.py:141
  171.3 9.8 %copy-start.10 = (bf16[128,1792]{1,0:T(8,128)(2,1)}, bf16[128,1792]{1,0:T(8,128)(2,1)S(1)}, u32[]{:S(2)}) copy-start(bf16[128,1792]{1,0:T(8,128)(2,1)S(1)} %collective-permute-done.14.refs_5_) | copy-start | bytes 1376260
  171.3 19.6 %collective-permute-start.15 = (bf16[128,1792]{1,0:T(8,128)(2,1)S(1)}, bf16[128,1792]{1,0:T(8,128)(2,1)}, u32[]{:S(2)}, u32[]{:S(2)}) collective-permute-start(bf16[128,1792]{1,0:T(8,128)(2,1)S(1)} %collective-permute-done.14.refs_5_), channel_id=1, source_target_pairs={{0,3},{1,0},{2,1},{3,2},{4,7},{5,4},{6,5},{7,6},{8,11},{9,8},{10,9... | collective-permute-start | bytes 1376264 | tf_op jit(solution)/shard_map/ppermute | solution.py:141
  195.6 27.2 %copy-start.21 = (f32[32,8]{0,1:T(8,128)S(1)}, f32[32,8]{0,1:T(8,128)}, u32[]{:S(2)}) copy-start(f32[32,8]{0,1:T(8,128)} %param.9) | copy-start | bytes 3076
  195.6 4.7 %collective-permute-start.20 = (bf16[256,256]{1,0:T(8,128)(2,1)}, bf16[256,256]{1,0:T(8,128)(2,1)S(1)}, u32[]{:S(2)}, u32[]{:S(2)}) collective-permute-start(bf16[256,256]{1,0:T(8,128)(2,1)} %shard_map.76.refs_0_), channel_id=1, source_target_pairs={{0,3},{1,0},{2,1},{3,2},{4,7},{5,4},{6,5},{7,6},{8,11},{9,8},{10,9... | collective-permute-start | bytes 393224 | tf_op jit(solution)/shard_map/ppermute | solution.py:141
  197.3 5.6 %collective-permute-start.19 = (bf16[256,256]{1,0:T(8,128)(2,1)}, bf16[256,256]{1,0:T(8,128)(2,1)S(1)}, u32[]{:S(2)}, u32[]{:S(2)}) collective-permute-start(bf16[256,256]{1,0:T(8,128)(2,1)} %shard_map.76.refs_0_), channel_id=1, source_target_pairs={{0,2},{1,3},{2,0},{3,1},{4,6},{5,7},{6,4},{7,5},{8,10},{9,11},{10,... | collective-permute-start | bytes 393224 | tf_op jit(solution)/shard_map/ppermute | solution.py:141
  197.3 7.5 %collective-permute-start.18 = (bf16[256,256]{1,0:T(8,128)(2,1)}, bf16[256,256]{1,0:T(8,128)(2,1)S(1)}, u32[]{:S(2)}, u32[]{:S(2)}) collective-permute-start(bf16[256,256]{1,0:T(8,128)(2,1)} %shard_map.76.refs_0_), channel_id=1, source_target_pairs={{0,1},{1,2},{2,3},{3,0},{4,5},{5,6},{6,7},{7,4},{8,9},{9,10},{10,1... | collective-permute-start | bytes 393224 | tf_op jit(solution)/shard_map/ppermute | solution.py:141
  210.2 38.3 %all-to-all-start.3 = ((bf16[64,4,1792]{2,1,0:T(4,128)(2,1)}), bf16[64,4,1792]{2,1,0:T(4,128)(2,1)S(1)}, u32[]{:S(2)}, u32[]{:S(2)}) async-start(bf16[64,4,1792]{2,1,0:T(4,128)(2,1)} %down.3), calls=%async_computation.3 | async-start | bytes 1835008 | tf_op jit(solution)/shard_map/all_to_all | solution.py:144
  (16 other events, 36.2 us)
